TPU v7x, 128 devices: a whole 4x4x4 slice. The times are simulated.
128 devices in a mesh: row: 16 (over z, x), col: 8 (over y, core).
Axes of the slice: x: 4, y: 4, z: 4, core: 2. Of those that a mesh axis runs over, the one named last changes fastest.
Arguments:
- density_first: bfloat16 [12288, 12288], P('row', 'col'), may hold values from -0.0068359375 to 0.0068359375
- density_second: bfloat16 [12288, 12288], P('row', 'col'), may hold values from -0.0068359375 to 0.0068359375
- basis: bfloat16 [256, 4096, 896], P(('row', 'col')), may hold values from -6 to 6
- tile_list: int32 [256, 7], P(('row', 'col')), may hold values from 0 to 95, as said below
- tile_count: int32 [256], P(('row', 'col')), may hold values from 5 to 7, as said below
- point_count: int32 [256], P(('row', 'col')), may hold values from 1024 to 4096, as said below
- offsets: float32 [3, 256, 4096], P(None, ('row', 'col')), may hold values from -5 to 5
- weights: float32 [256, 4096], P(('row', 'col')), may hold values from 0.05 to 1
- atom_of_point: int32 [256, 4096], P(('row', 'col')), may hold values from 0 to 1023, as said below
Outputs:
- density: float32 [2, 256, 4096], P(None, ('row', 'col'))
- moments: float32 [2, 9, 1024], replicated
Inputs may be any that keep to these rules, and one draw needn't show every extreme that they name: `tile_list`: the 7 tile numbers of each batch are 7 consecutive numbers in some order. `tile_count`: some batch has 7. `point_count`: some batch has 4096. `atom_of_point`: the points of batch g belong to atoms (g * 4 + j) mod 1024 with j from 0 to 7.
All inputs are finite; a program needn't handle non-finite values.
Results may differ from a plain program's by a relative error of at most 0.0003.
Values may be sent and summed in bfloat16 or wider, within the bound.
No kernel may reach another device: no remote copies, remote signals or barrier semaphores. Data moves between devices by JAX's collectives and lax.ppermute only.
A program may use at most 192 MiB of HBM per device.

v0:
```python
import jax
import jax.numpy as jnp
from jax import lax
from jax.experimental import pallas as pl
from jax.experimental.pallas import tpu as pltpu
from jax.sharding import Mesh
from jax.sharding import PartitionSpec as P

TILE = 128
KT = 7
NT = 96
PTS = 4096
ATOMS = 1024
N_ROW = 16
N_COL = 8
DEVICES = 128
SPAN = 12
ROW = ("row_0", "row_1")
COL = ("col_0", "col_1")
ROW_COL = ("row_0", "row_1", "col_0", "col_1")

SLOTS = 24
LINES = 32
PAIRS = KT * (KT + 1) // 2
WINDOW = 2 * PAIRS
FIRST = 32
REST = WINDOW - FIRST
FRONT = 1152
BACK = 1536
BLOCK = 512
STEPS = PTS // BLOCK
ROUNDER = 12582912.0


def pair_start(last):
    return last * (last + 1) // 2


def spread_body(place, own_start, first, second, out, tiles, lines, sems):
    my_row = place[0]
    my_col = place[1]
    lead = lax.rem(my_col - my_row + 16, 8)
    base = (my_row - my_col + lead) // 8
    copies = []
    for half in range(2):
        for step in range(6):
            for which, stored in enumerate((first, second)):
                index = which * 12 + half * 6 + step
                column = jnp.clip(2 * step + base - half, 0, 11)
                copy = pltpu.make_async_copy(
                    stored.at[pl.ds(step * TILE, TILE), pl.ds(pl.multiple_of(column * TILE, TILE), TILE)],
                    tiles.at[index],
                    sems.at[index],
                )
                copy.start()
                copies.append((copy, index, half, step))
    largest = jnp.zeros((8, TILE), jnp.float32)
    for copy, index, half, step in copies:
        copy.wait()
        values = tiles[index].astype(jnp.float32)
        column = 2 * step + base - half
        shift = lead - 8 * half
        used = (column >= 0) & (column < 12) & (shift <= 6) & (shift >= -6)
        peak = jnp.max(jnp.abs(values).reshape(16, 8, TILE), axis=0)
        largest = jnp.maximum(largest, jnp.where(used, peak, 0.0))
        if half:
            values = values.T
        lines[pl.ds(index, TILE, stride=SLOTS), :] = values
    peak = jnp.max(largest)
    line = lax.broadcasted_iota(jnp.int32, (8, TILE), 0)
    extra = jnp.where(
        line == 0,
        own_start[0].astype(jnp.float32),
        jnp.where(line == 1, own_start[1].astype(jnp.float32), peak),
    )

    def pack(dest, carry):
        at = pl.multiple_of(dest * SLOTS, 8)
        low = lines[pl.ds(at, 16), :]
        high = lines[pl.ds(at + 16, 8), :]
        to = pl.multiple_of(dest * LINES, 16)
        out[pl.ds(to, 16), :] = low.astype(jnp.bfloat16)
        out[pl.ds(to + 16, 16), :] = jnp.concatenate([high, extra], axis=0).astype(jnp.bfloat16)
        return carry

    lax.fori_loop(0, DEVICES, pack, 0, unroll=4)


def spread(place, own_start, first, second):
    return pl.pallas_call(
        spread_body,
        out_shape=jax.ShapeDtypeStruct((DEVICES * LINES, TILE), jnp.bfloat16),
        in_specs=[
            pl.BlockSpec(memory_space=pltpu.SMEM),
            pl.BlockSpec(memory_space=pltpu.SMEM),
            pl.BlockSpec(memory_space=pl.ANY),
            pl.BlockSpec(memory_space=pl.ANY),
        ],
        out_specs=pl.BlockSpec(memory_space=pltpu.VMEM),
        scratch_shapes=[
            pltpu.VMEM((SLOTS, TILE, TILE), jnp.bfloat16),
            pltpu.VMEM((DEVICES * SLOTS, TILE), jnp.float32),
            pltpu.SemaphoreType.DMA((SLOTS,)),
        ],
        name="spread_rows",
    )(place, own_start, first, second)


def window_body(arrived, out_first, out_rest, unit_out, lines, coded, start_lines, starts, sem):
    def widen(source, top):
        at = pl.multiple_of(source * LINES, 16)
        to = pl.multiple_of(FRONT + source * SLOTS, 8)
        low = arrived[pl.ds(at, 16), :].astype(jnp.float32)
        high = arrived[pl.ds(at + 16, 16), :].astype(jnp.float32)
        lines[pl.ds(to, 16), :] = low
        lines[pl.ds(to + 16, 8), :] = high[0:8]
        extra = high[8:16]
        peak, own = top
        lane = lax.broadcasted_iota(jnp.int32, (8, TILE), 1)
        own = jnp.where(lane == source, extra, own)
        return jnp.maximum(peak, extra), own

    zero = jnp.zeros((8, TILE), jnp.float32)
    tops, own = lax.fori_loop(0, DEVICES, widen, (zero, zero), unroll=4)
    start_lines[...] = own.astype(jnp.int32)
    copy = pltpu.make_async_copy(start_lines, starts, sem)
    copy.start()
    peak = jnp.broadcast_to(tops[2:3, :], (8, TILE))
    scale = jnp.full((8, TILE), 2.0**21, jnp.float32)
    unit = jnp.full((8, TILE), 2.0**-21, jnp.float32)
    for step in range(1, 64):
        small = peak < 2.0 ** (-7 - step)
        scale = jnp.where(small, 2.0 ** (21 + step), scale)
        unit = jnp.where(small, 2.0 ** (-21 - step), unit)
    unit_out[...] = unit

    order = lax.broadcasted_iota(jnp.int32, (8, TILE), 0)

    def line_of(row, col, which, half, step):
        return FRONT + (row * N_COL + col) * SLOTS + which * 12 + half * 6 + step

    def eight(start):
        return lines[pl.ds(start, 8, stride=(N_COL + 1) * SLOTS), :]

    for apart in range(KT):
        for group in range(NT // 8):
            words = []
            for which in range(2):
                odd = group % 2
                step = group // 2
                if odd or apart == 0:
                    total = eight(line_of(8 * odd - apart, 0, which, 0, step))
                else:
                    total = eight(line_of(-apart, 0, which, 0, step))
                    if step > 0:
                        before = eight(line_of(16 - apart, 0, which, 0, step - 1))
                        total = jnp.where(order < apart, before, total)
                if apart > 0:
                    after = eight(line_of(8 * odd, -apart, which, 1, step))
                    wrapped = eight(line_of(8 * odd, 8 - apart, which, 1, step))
                    total = total + jnp.where(order < apart, wrapped, after)
                total = total * scale
                words.append(((total + ROUNDER) - ROUNDER).astype(jnp.int32))
            word = (words[0] << 16) | (words[1] & 0xFFFF)
            coded[pl.ds(group * 64 + apart, 8, stride=8), :] = word

    copy.wait()

    def fill(dest, carry):
        for batch in range(2):
            begin = starts[batch, dest]
            for last in range(KT):
                words = coded[pl.ds(pl.multiple_of((begin + last) * 8, 8), 8), :]
                low = batch * PAIRS + pair_start(last)
                high = low + last + 1
                if low < FIRST:
                    cut = min(high, FIRST)
                    out_first[dest, low:cut, :] = words[0 : cut - low]
                if high > FIRST:
                    cut = max(low, FIRST)
                    out_rest[dest, cut - FIRST : high - FIRST, :] = words[cut - low : last + 1]
        return carry

    lax.fori_loop(0, DEVICES, fill, 0, unroll=2)


def windows(arrived):
    return pl.pallas_call(
        window_body,
        out_shape=(
            jax.ShapeDtypeStruct((DEVICES, FIRST, TILE), jnp.int32),
            jax.ShapeDtypeStruct((DEVICES, REST, TILE), jnp.int32),
            jax.ShapeDtypeStruct((8, TILE), jnp.float32),
        ),
        in_specs=[pl.BlockSpec(memory_space=pltpu.VMEM)],
        out_specs=tuple(pl.BlockSpec(memory_space=pltpu.VMEM) for _ in range(3)),
        scratch_shapes=[
            pltpu.VMEM((FRONT + DEVICES * SLOTS + BACK, TILE), jnp.float32),
            pltpu.VMEM((NT * 8, TILE), jnp.int32),
            pltpu.VMEM((8, TILE), jnp.int32),
            pltpu.SMEM((8, TILE), jnp.int32),
            pltpu.SemaphoreType.DMA,
        ],
        name="pick_windows",
    )(arrived)


def unit_at(batch, low, high):
    line = batch * PAIRS + pair_start(high) + (high - low)
    if line < FIRST:
        return 0, line
    return 1, line - FIRST


def batch_body(batch, table, *refs):
    data = refs[:2] if batch else (refs[0], None)
    refs = refs[2:] if batch else refs[1:]
    unit, offsets, weights, atoms = refs[:4]
    basis = refs[4 : 4 + KT]
    density, payload = refs[4 + KT : 6 + KT]
    high_part, low_part = refs[6 + KT :]
    step = pl.program_id(0)
    live_points = table[14]
    base_atom = table[15]

    @pl.when(step == 0)
    def _():
        zero = jnp.zeros((TILE, TILE), jnp.bfloat16)
        for last in range(KT):
            for first in range(last + 1):
                which, line = unit_at(batch, first, last)
                length = REST if which else FIRST
                words = data[which][pl.ds(line, TILE, stride=length), :]
                keep = table[7 + first] * table[7 + last]
                for matrix in range(2):
                    value = words >> 16 if matrix == 0 else (words << 16) >> 16
                    value = (value * keep).astype(jnp.float32)
                    top = value.astype(jnp.bfloat16)
                    rows = slice(first * TILE, (first + 1) * TILE)
                    at = (last + matrix * KT if last < KT - 1 else 12 + matrix) * TILE
                    if last < KT - 1:
                        at = (last + matrix * (KT - 1)) * TILE
                    high_part[rows, at : at + TILE] = top
                    if first < last:
                        bottom = (value - top.astype(jnp.float32)).astype(jnp.bfloat16)
                        low_part[rows, at : at + TILE] = bottom
        for matrix in range(2):
            for pair in range(3):
                at = (2 * pair + matrix * (KT - 1)) * TILE
                rows = slice((2 * pair + 1) * TILE, (2 * pair + 2) * TILE)
                high_part[rows, at : at + TILE] = zero
                rows = slice(2 * pair * TILE, (2 * pair + 1) * TILE)
                low_part[rows, at : at + TILE] = zero

    start = pl.multiple_of(step * BLOCK, BLOCK)

    @pl.when(start >= live_points)
    def _():
        density[:, pl.ds(start, BLOCK)] = jnp.zeros((2, BLOCK), jnp.float32)

    @pl.when(start < live_points)
    def _():
        columns = [ref[...] for ref in basis]
        values = jnp.concatenate(columns, axis=1)
        sums = [None, None]

        def product(at, tiles, top_rows, low_rows):
            ahead = jnp.dot(
                values[:, :top_rows], high_part[:top_rows, at : at + tiles * TILE],
                preferred_element_type=jnp.float32,
            )
            return ahead + jnp.dot(
                values[:, :low_rows], low_part[:low_rows, at : at + tiles * TILE],
                preferred_element_type=jnp.float32,
            )

        def add(matrix, part):
            sums[matrix] = part if sums[matrix] is None else sums[matrix] + part

        for pair in range(3):
            for matrix in range(2):
                at = (2 * pair + matrix * (KT - 1)) * TILE
                got = product(at, 2, (2 * pair + 2) * TILE, (2 * pair + 1) * TILE)
                add(matrix, got[:, :TILE] * columns[2 * pair].astype(jnp.float32))
                add(matrix, got[:, TILE:] * columns[2 * pair + 1].astype(jnp.float32))
        got = product(12 * TILE, 2, KT * TILE, (KT - 1) * TILE)
        last = columns[KT - 1].astype(jnp.float32)
        add(0, got[:, :TILE] * last)
        add(1, got[:, TILE:] * last)
        point = start + lax.broadcasted_iota(jnp.int32, (1, BLOCK), 1)
        scale = jnp.where(point < live_points, unit[0:1, 0:1], 0.0)
        for matrix in range(2):
            line = jnp.concatenate(
                [
                    jnp.sum(sums[matrix][cut : cut + TILE].T, axis=0, keepdims=True)
                    for cut in range(0, BLOCK, TILE)
                ],
                axis=1,
            )
            density[matrix : matrix + 1, pl.ds(start, BLOCK)] = line * scale

    @pl.when(step == STEPS - 1)
    def _():
        x = offsets[0, batch : batch + 1, :]
        y = offsets[1, batch : batch + 1, :]
        z = offsets[2, batch : batch + 1, :]
        weight = weights[batch : batch + 1, :]
        near = lax.rem(atoms[batch : batch + 1, :] - base_atom + 2 * ATOMS, ATOMS)
        squared = x * x + y * y + z * z
        shapes = [
            jnp.ones_like(x), x, y, z, x * y, y * z,
            3.0 * z * z - squared, x * z, x * x - y * y,
        ]
        shapes = jnp.concatenate([weight * shape for shape in shapes], axis=0)
        lane = lax.broadcasted_iota(jnp.int32, (9, TILE), 1)
        degree = lax.broadcasted_iota(jnp.int32, (9, TILE), 0)
        lane = lane - degree * SPAN
        for matrix in range(2):
            terms = density[matrix : matrix + 1, :] * shapes
            total = jnp.zeros((9, TILE), jnp.float32)
            for atom in range(8):
                picked = jnp.sum(jnp.where(near == atom, terms, 0.0), axis=1, keepdims=True)
                total = total + jnp.where(lane == atom + 4 * batch, picked, 0.0)
            payload[matrix : matrix + 1, :] = jnp.sum(total, axis=0, keepdims=True)


def batch_call(batch, table, data, unit, offsets, weights, atoms, basis):
    def whole(array):
        return pl.BlockSpec(array.shape, lambda i, t, n=array.ndim: (0,) * n)

    def column(place):
        def index(i, t):
            top = jnp.maximum(t[14] - 1, 0) // BLOCK
            return (batch * STEPS + jnp.minimum(i, top), t[place])

        return pl.BlockSpec((BLOCK, TILE), index)

    arrays = [*data, unit, offsets, weights, atoms]
    spec = pltpu.PrefetchScalarGridSpec(
        num_scalar_prefetch=1,
        grid=(STEPS,),
        in_specs=[whole(array) for array in arrays] + [column(place) for place in range(KT)],
        out_specs=(
            pl.BlockSpec((2, PTS), lambda i, t: (0, 0)),
            pl.BlockSpec((2, TILE), lambda i, t: (0, 0)),
        ),
        scratch_shapes=[
            pltpu.VMEM((KT * TILE, 14 * TILE), jnp.bfloat16),
            pltpu.VMEM((KT * TILE, 14 * TILE), jnp.bfloat16),
        ],
    )

    def body(*refs):
        batch_body(batch, *refs)

    return pl.pallas_call(
        body,
        grid_spec=spec,
        out_shape=(
            jax.ShapeDtypeStruct((2, PTS), jnp.float32),
            jax.ShapeDtypeStruct((2, TILE), jnp.float32),
        ),
        compiler_params=pltpu.CompilerParams(vmem_limit_bytes=60 * 1024 * 1024),
        cost_estimate=pl.CostEstimate(
            flops=26_000_000_000, bytes_accessed=10_000_000, transcendentals=0
        ),
        name=f"batch_density_{batch}",
    )(table, *arrays, *([basis] * KT))


def moment_body(arrived, out):
    lane = lax.broadcasted_iota(jnp.int32, (8, TILE), 1)
    for matrix in range(2):
        totals = [jnp.zeros((8, TILE), jnp.float32) for _ in range(9)]
        for place in range(16):
            part = arrived[pl.ds(2 * place + matrix, 8, stride=32), :]
            for degree in range(9):
                moved = pltpu.roll(part, (8 * place - SPAN * degree) % TILE, 1)
                if place < 15:
                    mine = (lane >= 8 * place) & (lane < 8 * place + SPAN)
                    totals[degree] = totals[degree] + jnp.where(mine, moved, 0.0)
                else:
                    inside = jnp.where(lane >= 8 * place, moved, 0.0)
                    after = pltpu.roll(jnp.where(lane < SPAN - 8, moved, 0.0), 1, 0)
                    totals[degree] = totals[degree] + inside + after
        for degree in range(9):
            for block in range(8):
                out[matrix, degree : degree + 1, block * TILE : (block + 1) * TILE] = totals[degree][
                    block : block + 1, :
                ]


def moment_table(arrived):
    return pl.pallas_call(
        moment_body,
        out_shape=jax.ShapeDtypeStruct((2, 9, ATOMS), jnp.float32),
        in_specs=[pl.BlockSpec(memory_space=pltpu.VMEM)],
        out_specs=pl.BlockSpec(memory_space=pltpu.VMEM),
        name="moment_table",
    )(arrived)


def exchange(value):
    return lax.all_to_all(value, ROW_COL, 0, 0, tiled=True)


def local(
    density_first,
    density_second,
    basis,
    tile_list,
    tile_count,
    point_count,
    offsets,
    weights,
    atom_of_point,
):
    my_row = lax.axis_index(ROW)
    my_col = lax.axis_index(COL)
    device = my_row * N_COL + my_col
    own_start = jnp.min(tile_list, axis=1)
    place = jnp.stack([my_row, my_col]).astype(jnp.int32)
    rows = spread(place, own_start, density_first, density_second)
    rows = exchange(rows.reshape(DEVICES, LINES, TILE)).reshape(DEVICES * LINES, TILE)
    first, rest, unit = windows(rows)
    first = exchange(first).reshape(DEVICES * FIRST, TILE)
    rest = exchange(rest).reshape(DEVICES * REST, TILE)

    relative = tile_list - own_start[:, None]
    hit = relative[:, None, :] == jnp.arange(KT, dtype=jnp.int32)[None, :, None]
    column = jnp.sum(jnp.where(hit, jnp.arange(KT, dtype=jnp.int32)[None, None, :], 0), axis=2)
    live = (column < tile_count[:, None]).astype(jnp.int32)
    first_atom = (2 * device + jnp.arange(2, dtype=jnp.int32)) * 4 % ATOMS
    table = jnp.concatenate(
        [column, live, point_count[:, None], first_atom[:, None].astype(jnp.int32)], axis=1
    ).astype(jnp.int32)
    flat = basis.reshape(-1, KT * TILE)
    side = (unit, offsets, weights, atom_of_point)
    density_0, payload_0 = batch_call(0, table[0], (first,), *side, flat)
    density_1, payload_1 = batch_call(1, table[1], (first, rest), *side, flat)
    density = jnp.stack([density_0, density_1], axis=1)
    payload = payload_0 + payload_1
    spread_out = jnp.broadcast_to(payload[None], (DEVICES, 2, TILE))
    moments = moment_table(exchange(spread_out).reshape(DEVICES * 2, TILE))
    return density, moments


def solution(mesh):
    torus = Mesh(mesh.devices.reshape(4, 4, 4, 2), ("row_0", "row_1", "col_0", "col_1"))
    in_specs = (
        P(ROW, COL),
        P(ROW, COL),
        P(ROW_COL, None, None),
        P(ROW_COL, None),
        P(ROW_COL),
        P(ROW_COL),
        P(None, ROW_COL, None),
        P(ROW_COL, None),
        P(ROW_COL, None),
    )
    out_specs = (P(None, ROW_COL, None), P())
    return jax.shard_map(local, mesh=torus, in_specs=in_specs, out_specs=out_specs, check_vma=False)
```

profile of v0, /device:TPU:1, one launch (start us, length us, event | category | flops | bytes accessed | tf_op | source)
XLA Modules:
  0.0 161.3 jit_solution(7723108739068770965)
XLA Ops:
  0.6 1.4 reduce_min.9.own_start
  2.0 0.7 pad_add_fusion.1.place
  2.7 4.6 %spread_rows.1 = bf16[4096,128]{1,0:T(8,128)(2,1)} custom-call(s32[2]{0:T(128)} %pad_add_fusion.1.place, s32[2]{0:T(128)} %reduce_min.9.own_start, bf16[768,1536]{1,0:T(8,128)(2,1)} %first.1, bf16[768,1536]{1,0:T(8,128)(2,1)} %second.1), custom_call_target="tpu_custom_call" | custom-call | tf_op jit(solution)/shard_map/spread_rows/pallas_call | solution.py:90
  7.3 30.4 %all_to_all.20 = bf16[128,32,128]{2,1,0:T(8,128)(2,1)} all-to-all(bf16[128,32,128]{2,1,0:T(8,128)(2,1)} %bitcast.32), channel_id=1, replica_groups=mesh['row_0'=4,'row_1'=4,'col_0'=4,'col_1'=2] {'row_0','row_1','col_0','..., dimensions={0} | all-to-all | bytes 2097152 | tf_op jit(solution)/shard_map/all_to_all | solution.py:404
  37.7 5.2 %pick_windows.1 = (s32[128,32,128]{2,1,0:T(8,128)}, s32[128,24,128]{2,1,0:T(8,128)}, f32[8,128]{1,0:T(8,128)}) custom-call(bf16[4096,128]{1,0:T(8,128)(2,1)} %bitcast.31), custom_call_target="tpu_custom_call" | custom-call | tf_op jit(solution)/shard_map/pick_windows/pallas_call | solution.py:188
  42.9 0.0 copy-start.7
  42.9 0.0 copy-start.3
  42.9 0.0 copy-start.4
  42.9 0.0 copy-start.6
  42.9 4.8 %all-to-all-start.1 = ((s32[128,32,128]{2,1,0:T(8,128)}), s32[128,32,128]{2,1,0:T(8,128)S(1)}, u32[]{:S(2)}, u32[]{:S(2)}) async-start(s32[128,32,128]{2,1,0:T(8,128)} %get-tuple-element.9), calls=%async_computation.1 | async-start | bytes 4194304 | tf_op jit(solution)/shard_map/all_to_all | solution.py:404
  47.7 0.0 copy-done.7
  47.7 0.1 copy.20
  47.8 0.0 copy-done.3
  47.8 0.0 copy-done.4
  47.8 0.1 broadcast_subtract_fusion
  47.9 0.2 fusion
  48.1 0.1 copy.18
  48.2 0.0 copy-done.6
  48.2 0.1 copy.19
  48.3 0.1 pad_add_fusion
  48.4 0.5 slice_bitcast_fusion.1
  49.0 29.0 %all-to-all-done.1 = s32[128,32,128]{2,1,0:T(8,128)S(1)} async-done(((s32[128,32,128]{2,1,0:T(8,128)}), s32[128,32,128]{2,1,0:T(8,128)S(1)}, u32[]{:S(2)}, u32[]{:S(2)}) %all-to-all-start.1) | async-done | bytes 2097184 | tf_op jit(solution)/shard_map/all_to_all | solution.py:404
  78.0 0.0 copy-start
  78.0 5.8 %all-to-all-start.2 = ((s32[128,24,128]{2,1,0:T(8,128)}), s32[128,24,128]{2,1,0:T(8,128)}, u32[]{:S(2)}, u32[]{:S(2)}) async-start(s32[128,24,128]{2,1,0:T(8,128)} %get-tuple-element.12), calls=%async_computation.2 | async-start | bytes 3145728 | tf_op jit(solution)/shard_map/all_to_all | solution.py:404
  83.8 0.0 copy-done
  83.8 24.1 %batch_density_0.1 = (f32[2,4096]{1,0:T(2,128)}, f32[2,128]{1,0:T(2,128)}) custom-call(s32[16]{0:T(128)} %get-tuple-element.24.refs_0_, s32[4096,128]{1,0:T(8,128)} %bitcast.29, f32[8,128]{1,0:T(8,128)} %get-tuple-element.10.refs_2_.refs_3_, f32[3,2,4096]{2,1,0:T(2,128)} %refs_4_.3, f32[2,4096]{1,0:T(2,128)} %refs_5_.3, s32[2,4096]{1,0:T(2,128)} %refs_6_.1, ...), custom_call_target="tpu_custom_call" | custom-call | flops 25999998976 | bytes 10000000 | tf_op jit(solution)/shard_map/batch_density_0/pallas_call | solution.py:356
  107.9 0.1 all-to-all-done.2
  108.0 0.0 copy-start.5
  108.0 0.0 copy-start.2
  108.0 21.2 %batch_density_1.1 = (f32[2,4096]{1,0:T(2,128)}, f32[2,128]{1,0:T(2,128)}) custom-call(s32[16]{0:T(128)} %get-tuple-element.25.refs_0_, s32[4096,128]{1,0:T(8,128)} %bitcast.30, s32[3072,128]{1,0:T(8,128)} %bitcast.10.refs_2_, f32[8,128]{1,0:T(8,128)} %get-tuple-element.10.refs_2_.refs_3_, f32[3,2,4096]{2,1,0:T(2,128)} %refs_4_.3, f32[2,4096]{1,0:T(2,128)} %refs_5_.3, ...), custom_call_target="tpu_custom_call" | custom-call | flops 25999998976 | bytes 10000000 | tf_op jit(solution)/shard_map/batch_density_1/pallas_call | solution.py:356
  129.2 0.0 copy-done.5
  129.2 0.7 add.44
  129.9 0.7 broadcast_in_dim.30
  130.6 16.5 %all-to-all-start.3 = ((f32[128,2,128]{2,1,0:T(2,128)}), f32[128,2,128]{2,1,0:T(2,128)S(1)}, u32[]{:S(2)}, u32[]{:S(2)}) async-start(f32[128,2,128]{2,1,0:T(2,128)} %broadcast_in_dim.30), calls=%async_computation.3 | async-start | bytes 262144 | tf_op jit(solution)/shard_map/all_to_all | solution.py:404
  147.1 0.0 copy-done.2
  147.1 0.8 pad_maximum_fusion
  147.9 0.7 copy.21
  148.6 8.5 %all-to-all-done.3 = f32[128,2,128]{2,1,0:T(2,128)S(1)} async-done(((f32[128,2,128]{2,1,0:T(2,128)}), f32[128,2,128]{2,1,0:T(2,128)S(1)}, u32[]{:S(2)}, u32[]{:S(2)}) %all-to-all-start.3) | async-done | bytes 131104 | tf_op jit(solution)/shard_map/all_to_all | solution.py:404
  157.1 0.0 copy-start.1
  157.1 0.6 copy-done.1
  157.8 1.9 %moment_table.1 = f32[2,9,1024]{2,1,0:T(8,128)} custom-call(f32[256,128]{1,0:T(8,128)} %bitcast.33), custom_call_target="tpu_custom_call" | custom-call | tf_op jit(solution)/shard_map/moment_table/pallas_call | solution.py:394
  159.7 1.6 copy.22
  (2 shorter events, 0.0 us)
Async XLA Ops:
  42.9 4.9 %copy-start.7 = (s32[2]{0:T(128)S(1)}, s32[2]{0:T(128)}, u32[]{:S(2)}) copy-start(s32[2]{0:T(128)} %param.14) | copy-start | bytes 28
  42.9 5.0 %copy-start.3 = (s32[2]{0:T(128)S(1)}, s32[2]{0:T(128)}, u32[]{:S(2)}) copy-start(s32[2]{0:T(128)} %reduce_min.9.own_start) | copy-start | bytes 28
  42.9 5.0 %copy-start.4 = (s32[2,7]{1,0:T(2,128)S(1)}, s32[2,7]{1,0:T(2,128)}, u32[]{:S(2)}) copy-start(s32[2,7]{1,0:T(2,128)} %param.12) | copy-start | bytes 172
  42.9 5.3 %copy-start.6 = (s32[2]{0:T(128)S(1)}, s32[2]{0:T(128)}, u32[]{:S(2)}) copy-start(s32[2]{0:T(128)} %param.13) | copy-start | bytes 28
  42.9 35.1 %all-to-all-start.1 = ((s32[128,32,128]{2,1,0:T(8,128)}), s32[128,32,128]{2,1,0:T(8,128)S(1)}, u32[]{:S(2)}, u32[]{:S(2)}) async-start(s32[128,32,128]{2,1,0:T(8,128)} %get-tuple-element.9), calls=%async_computation.1 | async-start | bytes 4194304 | tf_op jit(solution)/shard_map/all_to_all | solution.py:404
  78.0 5.8 %copy-start = (s32[128,32,128]{2,1,0:T(8,128)}, s32[128,32,128]{2,1,0:T(8,128)S(1)}, u32[]{:S(2)}) copy-start(s32[128,32,128]{2,1,0:T(8,128)S(1)} %all-to-all-done.1) | copy-start | bytes 6291460
  78.0 30.0 %all-to-all-start.2 = ((s32[128,24,128]{2,1,0:T(8,128)}), s32[128,24,128]{2,1,0:T(8,128)}, u32[]{:S(2)}, u32[]{:S(2)}) async-start(s32[128,24,128]{2,1,0:T(8,128)} %get-tuple-element.12), calls=%async_computation.2 | async-start | bytes 3145728 | tf_op jit(solution)/shard_map/all_to_all | solution.py:404
  108.0 21.3 %copy-start.5 = (f32[2,128]{1,0:T(2,128)S(1)}, f32[2,128]{1,0:T(2,128)}, u32[]{:S(2)}) copy-start(f32[2,128]{1,0:T(2,128)} %get-tuple-element.14) | copy-start | bytes 3076
  108.0 39.2 %copy-start.2 = (f32[2,4096]{1,0:T(2,128)S(1)}, f32[2,4096]{1,0:T(2,128)}, u32[]{:S(2)}) copy-start(f32[2,4096]{1,0:T(2,128)} %get-tuple-element.11) | copy-start | bytes 98308
  130.6 26.5 %all-to-all-start.3 = ((f32[128,2,128]{2,1,0:T(2,128)}), f32[128,2,128]{2,1,0:T(2,128)S(1)}, u32[]{:S(2)}, u32[]{:S(2)}) async-start(f32[128,2,128]{2,1,0:T(2,128)} %broadcast_in_dim.30), calls=%async_computation.3 | async-start | bytes 262144 | tf_op jit(solution)/shard_map/all_to_all | solution.py:404
  157.1 0.7 copy-start.1
where the time goes:
time: 162 us; the launch traced here: 161 us
  Pallas kernels  57.1 us (35%)
  waiting for transfers between devices  37.6 us (23%)
  blocking collectives  30.4 us (19%)
  starting transfers between devices  27.1 us (17%)
  local copies, waits for them, and re-layouts  4.47 us (3%)
  other arithmetic  3.9 us (2%)
    pallas_call x2, Pallas kernels, batch_call(): pl.pallas_call(body, grid_spec=spec, out_shape=(jax.ShapeDtypeStruct((2,...  45.4 us
    all_to_all x3, waiting for transfers between devices, exchange(): return lax.all_to_all(value, ROW_COL, 0, 0, tiled=True)  37.6 us
    all_to_all x1, blocking collectives, exchange(): return lax.all_to_all(value, ROW_COL, 0, 0, tiled=True)  30.4 us
    all_to_all x3, starting transfers between devices, exchange(): return lax.all_to_all(value, ROW_COL, 0, 0, tiled=True)  27.1 us
    pallas_call x1, Pallas kernels, windows(): pl.pallas_call(window_body, out_shape=(jax.ShapeDtypeStruct((DEVICES, FIR...  5.18 us
    pallas_call x1, Pallas kernels, spread(): pl.pallas_call(spread_body, out_shape=jax.ShapeDtypeStruct((DEVICES * LIN...  4.59 us
  transfers between devices with their start and end apart: 3, of which 3 were waited for; matrix products, arithmetic and copies ran while one was open for 2% of the time, Pallas kernels for 15%

commit v1 on v0

--- a/solution.py
+++ b/solution.py
@@ -36,9 +36,15 @@
     return last * (last + 1) // 2
 
 
-def spread_body(place, own_start, first, second, out, tiles, lines, sems):
-    my_row = place[0]
-    my_col = place[1]
+def spread_body(tile_list, first, second, out, tiles, lines, sems):
+    my_row = lax.axis_index(ROW)
+    my_col = lax.axis_index(COL)
+    own_start = []
+    for batch in range(2):
+        least = tile_list[batch, 0]
+        for place in range(1, KT):
+            least = jnp.minimum(least, tile_list[batch, place])
+        own_start.append(least)
     lead = lax.rem(my_col - my_row + 16, 8)
     base = (my_row - my_col + lead) // 8
     copies = []
@@ -86,12 +92,11 @@
     lax.fori_loop(0, DEVICES, pack, 0, unroll=4)
 
 
-def spread(place, own_start, first, second):
+def spread(tile_list, first, second):
     return pl.pallas_call(
         spread_body,
         out_shape=jax.ShapeDtypeStruct((DEVICES * LINES, TILE), jnp.bfloat16),
         in_specs=[
-            pl.BlockSpec(memory_space=pltpu.SMEM),
             pl.BlockSpec(memory_space=pltpu.SMEM),
             pl.BlockSpec(memory_space=pl.ANY),
             pl.BlockSpec(memory_space=pl.ANY),
@@ -103,7 +108,7 @@
             pltpu.SemaphoreType.DMA((SLOTS,)),
         ],
         name="spread_rows",
-    )(place, own_start, first, second)
+    )(tile_list, first, second)
 
 
 def window_body(arrived, out_first, out_rest, unit_out, lines, coded, start_lines, starts, sem):
@@ -205,6 +210,30 @@
     )(arrived)
 
 
+def table_body(tile_list, tile_count, point_count, table):
+    device = lax.axis_index(ROW) * N_COL + lax.axis_index(COL)
+    for batch in range(2):
+        start = tile_list[batch, 0]
+        for place in range(1, KT):
+            start = jnp.minimum(start, tile_list[batch, place])
+        for place in range(KT):
+            rank = tile_list[batch, place] - start
+            table[batch * 16 + rank] = place
+            table[batch * 16 + KT + rank] = (place < tile_count[batch]).astype(jnp.int32)
+        table[batch * 16 + 14] = point_count[batch]
+        table[batch * 16 + 15] = lax.rem((2 * device + batch) * 4, ATOMS)
+
+
+def batch_tables(tile_list, tile_count, point_count):
+    return pl.pallas_call(
+        table_body,
+        out_shape=jax.ShapeDtypeStruct((32,), jnp.int32),
+        in_specs=[pl.BlockSpec(memory_space=pltpu.SMEM) for _ in range(3)],
+        out_specs=pl.BlockSpec(memory_space=pltpu.SMEM),
+        name="batch_tables",
+    )(tile_list, tile_count, point_count)
+
+
 def unit_at(batch, low, high):
     line = batch * PAIRS + pair_start(high) + (high - low)
     if line < FIRST:
@@ -212,92 +241,103 @@
     return 1, line - FIRST
 
 
+def first_blocks(batch):
+    begin = batch * PAIRS // 8
+    return range(begin, min(-(-(batch + 1) * PAIRS // 8), FIRST // 8))
+
+
 def batch_body(batch, table, *refs):
-    data = refs[:2] if batch else (refs[0], None)
-    refs = refs[2:] if batch else refs[1:]
+    first_count = len(first_blocks(batch))
+    first_rows = refs[:first_count]
+    refs = refs[first_count:]
+
+    def from_first(line):
+        rows = first_rows[line // 8 - first_blocks(batch)[0]].reshape(DEVICES * 8, TILE)
+        return rows[pl.ds(line % 8, TILE, stride=8), :]
+
+    if batch:
+        rest_rows = refs[0]
+        before = refs[1]
+        earlier = refs[2]
+        refs = refs[3:]
+
+        def from_rest(line):
+            return rest_rows[pl.ds(line, TILE, stride=REST), :]
+
+        data = (from_first, from_rest)
+    else:
+        data = (from_first, None)
     unit, offsets, weights, atoms = refs[:4]
     basis = refs[4 : 4 + KT]
     density, payload = refs[4 + KT : 6 + KT]
     high_part, low_part = refs[6 + KT :]
     step = pl.program_id(0)
-    live_points = table[14]
-    base_atom = table[15]
+    live_points = table[batch * 16 + 14]
+    base_atom = table[batch * 16 + 15]
 
     @pl.when(step == 0)
     def _():
-        zero = jnp.zeros((TILE, TILE), jnp.bfloat16)
         for last in range(KT):
             for first in range(last + 1):
                 which, line = unit_at(batch, first, last)
-                length = REST if which else FIRST
-                words = data[which][pl.ds(line, TILE, stride=length), :]
-                keep = table[7 + first] * table[7 + last]
+                words = data[which](line)
+                keep = table[batch * 16 + KT + first] * table[batch * 16 + KT + last]
+                rows = slice(first * TILE, (first + 1) * TILE)
                 for matrix in range(2):
                     value = words >> 16 if matrix == 0 else (words << 16) >> 16
                     value = (value * keep).astype(jnp.float32)
                     top = value.astype(jnp.bfloat16)
-                    rows = slice(first * TILE, (first + 1) * TILE)
-                    at = (last + matrix * KT if last < KT - 1 else 12 + matrix) * TILE
-                    if last < KT - 1:
-                        at = (last + matrix * (KT - 1)) * TILE
+                    at = (2 * last + matrix) * TILE
                     high_part[rows, at : at + TILE] = top
                     if first < last:
                         bottom = (value - top.astype(jnp.float32)).astype(jnp.bfloat16)
                         low_part[rows, at : at + TILE] = bottom
-        for matrix in range(2):
-            for pair in range(3):
-                at = (2 * pair + matrix * (KT - 1)) * TILE
-                rows = slice((2 * pair + 1) * TILE, (2 * pair + 2) * TILE)
-                high_part[rows, at : at + TILE] = zero
-                rows = slice(2 * pair * TILE, (2 * pair + 1) * TILE)
-                low_part[rows, at : at + TILE] = zero
 
     start = pl.multiple_of(step * BLOCK, BLOCK)
+
+    def put(start, lines):
+        if batch:
+            at = pl.ds(start, BLOCK)
+            for matrix in range(2):
+                both = [earlier[matrix : matrix + 1, at], lines[matrix : matrix + 1]]
+                density[matrix, :, at] = jnp.concatenate(both, axis=0)
+        else:
+            density[:, pl.ds(start, BLOCK)] = lines
 
     @pl.when(start >= live_points)
     def _():
-        density[:, pl.ds(start, BLOCK)] = jnp.zeros((2, BLOCK), jnp.float32)
+        put(start, jnp.zeros((2, BLOCK), jnp.float32))
 
     @pl.when(start < live_points)
     def _():
         columns = [ref[...] for ref in basis]
         values = jnp.concatenate(columns, axis=1)
         sums = [None, None]
-
-        def product(at, tiles, top_rows, low_rows):
-            ahead = jnp.dot(
-                values[:, :top_rows], high_part[:top_rows, at : at + tiles * TILE],
-                preferred_element_type=jnp.float32,
+        for last in range(KT):
+            cols = slice(2 * last * TILE, (2 * last + 2) * TILE)
+            rows = (last + 1) * TILE
+            got = jnp.dot(
+                values[:, :rows], high_part[:rows, cols], preferred_element_type=jnp.float32
             )
-            return ahead + jnp.dot(
-                values[:, :low_rows], low_part[:low_rows, at : at + tiles * TILE],
-                preferred_element_type=jnp.float32,
-            )
-
-        def add(matrix, part):
-            sums[matrix] = part if sums[matrix] is None else sums[matrix] + part
-
-        for pair in range(3):
+            if last:
+                rows = last * TILE
+                got = got + jnp.dot(
+                    values[:, :rows], low_part[:rows, cols], preferred_element_type=jnp.float32
+                )
+            column = columns[last].astype(jnp.float32)
             for matrix in range(2):
-                at = (2 * pair + matrix * (KT - 1)) * TILE
-                got = product(at, 2, (2 * pair + 2) * TILE, (2 * pair + 1) * TILE)
-                add(matrix, got[:, :TILE] * columns[2 * pair].astype(jnp.float32))
-                add(matrix, got[:, TILE:] * columns[2 * pair + 1].astype(jnp.float32))
-        got = product(12 * TILE, 2, KT * TILE, (KT - 1) * TILE)
-        last = columns[KT - 1].astype(jnp.float32)
-        add(0, got[:, :TILE] * last)
-        add(1, got[:, TILE:] * last)
+                part = got[:, matrix * TILE : (matrix + 1) * TILE] * column
+                sums[matrix] = part if last == 0 else sums[matrix] + part
         point = start + lax.broadcasted_iota(jnp.int32, (1, BLOCK), 1)
         scale = jnp.where(point < live_points, unit[0:1, 0:1], 0.0)
+        lines = []
         for matrix in range(2):
-            line = jnp.concatenate(
-                [
-                    jnp.sum(sums[matrix][cut : cut + TILE].T, axis=0, keepdims=True)
-                    for cut in range(0, BLOCK, TILE)
-                ],
-                axis=1,
-            )
-            density[matrix : matrix + 1, pl.ds(start, BLOCK)] = line * scale
+            pieces = [
+                jnp.sum(sums[matrix][cut : cut + TILE].T, axis=0, keepdims=True)
+                for cut in range(0, BLOCK, TILE)
+            ]
+            lines.append(jnp.concatenate(pieces, axis=1) * scale)
+        put(start, jnp.concatenate(lines, axis=0))
 
     @pl.when(step == STEPS - 1)
     def _():
@@ -316,12 +356,20 @@
         degree = lax.broadcasted_iota(jnp.int32, (9, TILE), 0)
         lane = lane - degree * SPAN
         for matrix in range(2):
-            terms = density[matrix : matrix + 1, :] * shapes
+            if batch:
+                terms = density[matrix, batch : batch + 1, :] * shapes
+            else:
+                terms = density[matrix : matrix + 1, :] * shapes
             total = jnp.zeros((9, TILE), jnp.float32)
             for atom in range(8):
                 picked = jnp.sum(jnp.where(near == atom, terms, 0.0), axis=1, keepdims=True)
                 total = total + jnp.where(lane == atom + 4 * batch, picked, 0.0)
-            payload[matrix : matrix + 1, :] = jnp.sum(total, axis=0, keepdims=True)
+            line = jnp.sum(total, axis=0, keepdims=True)
+            if batch:
+                line = line + before[matrix : matrix + 1, :]
+                payload[:, matrix : matrix + 1, :] = jnp.broadcast_to(line[None], (DEVICES, 1, TILE))
+            else:
+                payload[matrix : matrix + 1, :] = line
 
 
 def batch_call(batch, table, data, unit, offsets, weights, atoms, basis):
@@ -330,23 +378,31 @@
 
     def column(place):
         def index(i, t):
-            top = jnp.maximum(t[14] - 1, 0) // BLOCK
-            return (batch * STEPS + jnp.minimum(i, top), t[place])
+            top = jnp.maximum(t[batch * 16 + 14] - 1, 0) // BLOCK
+            return (batch * STEPS + jnp.minimum(i, top), t[batch * 16 + place])
 
         return pl.BlockSpec((BLOCK, TILE), index)
 
-    arrays = [*data, unit, offsets, weights, atoms]
+    blocks = first_blocks(batch)
+    rest = [*data[1:], unit, offsets, weights, atoms]
+    arrays = [data[0]] * len(blocks) + rest
+    specs = [
+        pl.BlockSpec((DEVICES, 8, TILE), lambda i, t, block=block: (0, block, 0)) for block in blocks
+    ]
+    specs += [whole(array) for array in rest]
+    payload = (DEVICES, 2, TILE) if batch else (2, TILE)
+    density = (2, 2, PTS) if batch else (2, PTS)
     spec = pltpu.PrefetchScalarGridSpec(
         num_scalar_prefetch=1,
         grid=(STEPS,),
-        in_specs=[whole(array) for array in arrays] + [column(place) for place in range(KT)],
+        in_specs=specs + [column(place) for place in range(KT)],
         out_specs=(
-            pl.BlockSpec((2, PTS), lambda i, t: (0, 0)),
-            pl.BlockSpec((2, TILE), lambda i, t: (0, 0)),
+            pl.BlockSpec(density, lambda i, t: (0,) * len(density)),
+            pl.BlockSpec(payload, lambda i, t: (0,) * len(payload)),
         ),
         scratch_shapes=[
-            pltpu.VMEM((KT * TILE, 14 * TILE), jnp.bfloat16),
-            pltpu.VMEM((KT * TILE, 14 * TILE), jnp.bfloat16),
+            pltpu.VMEM((KT * TILE, 2 * KT * TILE), jnp.bfloat16),
+            pltpu.VMEM(((KT - 1) * TILE, 2 * KT * TILE), jnp.bfloat16),
         ],
     )
 
@@ -357,8 +413,8 @@
         body,
         grid_spec=spec,
         out_shape=(
-            jax.ShapeDtypeStruct((2, PTS), jnp.float32),
-            jax.ShapeDtypeStruct((2, TILE), jnp.float32),
+            jax.ShapeDtypeStruct(density, jnp.float32),
+            jax.ShapeDtypeStruct(payload, jnp.float32),
         ),
         compiler_params=pltpu.CompilerParams(vmem_limit_bytes=60 * 1024 * 1024),
         cost_estimate=pl.CostEstimate(
@@ -385,7 +441,7 @@
                     totals[degree] = totals[degree] + inside + after
         for degree in range(9):
             for block in range(8):
-                out[matrix, degree : degree + 1, block * TILE : (block + 1) * TILE] = totals[degree][
+                out[degree, matrix : matrix + 1, block * TILE : (block + 1) * TILE] = totals[degree][
                     block : block + 1, :
                 ]
 
@@ -393,7 +449,7 @@
 def moment_table(arrived):
     return pl.pallas_call(
         moment_body,
-        out_shape=jax.ShapeDtypeStruct((2, 9, ATOMS), jnp.float32),
+        out_shape=jax.ShapeDtypeStruct((9, 2, ATOMS), jnp.float32),
         in_specs=[pl.BlockSpec(memory_space=pltpu.VMEM)],
         out_specs=pl.BlockSpec(memory_space=pltpu.VMEM),
         name="moment_table",
@@ -415,33 +471,23 @@
     weights,
     atom_of_point,
 ):
-    my_row = lax.axis_index(ROW)
-    my_col = lax.axis_index(COL)
-    device = my_row * N_COL + my_col
-    own_start = jnp.min(tile_list, axis=1)
-    place = jnp.stack([my_row, my_col]).astype(jnp.int32)
-    rows = spread(place, own_start, density_first, density_second)
+    rows = spread(tile_list, density_first, density_second)
     rows = exchange(rows.reshape(DEVICES, LINES, TILE)).reshape(DEVICES * LINES, TILE)
     first, rest, unit = windows(rows)
-    first = exchange(first).reshape(DEVICES * FIRST, TILE)
-    rest = exchange(rest).reshape(DEVICES * REST, TILE)
-
-    relative = tile_list - own_start[:, None]
-    hit = relative[:, None, :] == jnp.arange(KT, dtype=jnp.int32)[None, :, None]
-    column = jnp.sum(jnp.where(hit, jnp.arange(KT, dtype=jnp.int32)[None, None, :], 0), axis=2)
-    live = (column < tile_count[:, None]).astype(jnp.int32)
-    first_atom = (2 * device + jnp.arange(2, dtype=jnp.int32)) * 4 % ATOMS
-    table = jnp.concatenate(
-        [column, live, point_count[:, None], first_atom[:, None].astype(jnp.int32)], axis=1
-    ).astype(jnp.int32)
+    with jax.named_scope("send_first"):
+        first = exchange(first)
+    with jax.named_scope("send_rest"):
+        rest = exchange(rest)
+
+    table = batch_tables(tile_list, tile_count, point_count)
     flat = basis.reshape(-1, KT * TILE)
     side = (unit, offsets, weights, atom_of_point)
-    density_0, payload_0 = batch_call(0, table[0], (first,), *side, flat)
-    density_1, payload_1 = batch_call(1, table[1], (first, rest), *side, flat)
-    density = jnp.stack([density_0, density_1], axis=1)
-    payload = payload_0 + payload_1
-    spread_out = jnp.broadcast_to(payload[None], (DEVICES, 2, TILE))
-    moments = moment_table(exchange(spread_out).reshape(DEVICES * 2, TILE))
+    density_0, payload_0 = batch_call(
+        0, table, (first,), *side, flat
+    )
+    rest = rest.reshape(DEVICES * REST, TILE)
+    density, payload = batch_call(1, table, (first, rest, payload_0, density_0), *side, flat)
+    moments = moment_table(exchange(payload).reshape(DEVICES * 2, TILE)).swapaxes(0, 1)
     return density, moments
 
 

time: 162 us -> 149 us (0.920)
  blocking collectives: 30.4 us -> 49.4 us
  starting transfers between devices: 27.1 us -> 10.6 us
  waiting for transfers between devices: 37.6 us -> 29.7 us
  local copies, waits for them, and re-layouts: 4.47 us -> 0.01 us
  other arithmetic: 3.9 us -> 0 us
    all_to_all x1 -> x2, blocking collectives: 30.4 us -> 49.4 us  [exchange(): return lax.all_to_all(value, ROW_COL, 0, 0, tiled=True)]
    all_to_all x3 -> x2, starting transfers between devices: 27.1 us -> 10.6 us  [exchange(): return lax.all_to_all(value, ROW_COL, 0, 0, tiled=True)]
    all_to_all x3 -> x2, waiting for transfers between devices: 37.6 us -> 29.7 us  [exchange(): return lax.all_to_all(value, ROW_COL, 0, 0, tiled=True)]
    unnamed x18 -> x2, local copies, waits for them, and re-layouts: 2.96 us -> 0.01 us
    pallas_call x3 -> x4, Pallas kernels: 47.3 us -> 48.2 us  [the longest x2 45 us: batch_call(): pl.pallas_call(body, grid_spec=spec, out_shape=(jax.ShapeDtypeStruct(dens...]
  transfers between devices with their start and end apart: 3 -> 2, of which waited for: 3 -> 2; matrix products, arithmetic and copies ran while one was open for 2% -> 0% of each run, Pallas kernels for 15% -> 17%
where the time goes in v1:
time: 149 us; the launch traced here: 148 us
  Pallas kernels  58 us (39%)
  blocking collectives  49.4 us (33%)
  waiting for transfers between devices  29.7 us (20%)
  starting transfers between devices  10.6 us (7%)
    all_to_all x2, blocking collectives, exchange(): return lax.all_to_all(value, ROW_COL, 0, 0, tiled=True)  49.4 us
    pallas_call x2, Pallas kernels, batch_call(): pl.pallas_call(body, grid_spec=spec, out_shape=(jax.ShapeDtypeStruct(dens...  45 us
    all_to_all x2, waiting for transfers between devices, exchange(): return lax.all_to_all(value, ROW_COL, 0, 0, tiled=True)  29.7 us
    all_to_all x2, starting transfers between devices, exchange(): return lax.all_to_all(value, ROW_COL, 0, 0, tiled=True)  10.6 us
    pallas_call x1, Pallas kernels, windows(): pl.pallas_call(window_body, out_shape=(jax.ShapeDtypeStruct((DEVICES, FIR...  5.19 us
    pallas_call x1, Pallas kernels, spread(): pl.pallas_call(spread_body, out_shape=jax.ShapeDtypeStruct((DEVICES * LIN...  4.61 us
  transfers between devices with their start and end apart: 2, of which 2 were waited for; matrix products, arithmetic and copies ran while one was open for 0% of the time, Pallas kernels for 17%

profile of v1, /device:TPU:1, one launch (start us, length us, event | category | flops | bytes accessed | tf_op | source)
XLA Modules:
  0.0 148.3 jit_solution(16557851254238478995)
XLA Ops:
  0.6 4.6 %spread_rows.1 = bf16[4096,128]{1,0:T(8,128)(2,1)} custom-call(s32[2,7]{1,0:T(2,128)} %tile_list.3, bf16[768,1536]{1,0:T(8,128)(2,1)} %first.1, bf16[768,1536]{1,0:T(8,128)(2,1)} %second.1), custom_call_target="tpu_custom_call" | custom-call | tf_op jit(solution)/shard_map/spread_rows/pallas_call | solution.py:96
  5.2 30.4 %all_to_all.20 = bf16[128,32,128]{2,1,0:T(8,128)(2,1)} all-to-all(bf16[128,32,128]{2,1,0:T(8,128)(2,1)} %bitcast.21), channel_id=1, replica_groups=mesh['row_0'=4,'row_1'=4,'col_0'=4,'col_1'=2] {'row_0','row_1','col_0','..., dimensions={0} | all-to-all | bytes 2097152 | tf_op jit(solution)/shard_map/all_to_all | solution.py:460
  35.6 5.2 %pick_windows.1 = (s32[128,32,128]{2,1,0:T(8,128)}, s32[128,24,128]{2,1,0:T(8,128)}, f32[8,128]{1,0:T(8,128)}) custom-call(bf16[4096,128]{1,0:T(8,128)(2,1)} %bitcast.20), custom_call_target="tpu_custom_call" | custom-call | tf_op jit(solution)/shard_map/pick_windows/pallas_call | solution.py:193
  40.8 4.8 %all-to-all-start.1 = ((s32[128,32,128]{2,1,0:T(8,128)}), s32[128,32,128]{2,1,0:T(8,128)S(1)}, u32[]{:S(2)}, u32[]{:S(2)}) async-start(s32[128,32,128]{2,1,0:T(8,128)} %get-tuple-element.9), calls=%async_computation.1 | async-start | bytes 4194304 | tf_op jit(solution)/shard_map/send_first/all_to_all | solution.py:460
  45.7 1.3 batch_tables.1.refs_0_
  46.9 29.0 %all-to-all-done.1.refs_1_.refs_2_.refs_3_.refs_4_ = s32[128,32,128]{2,1,0:T(8,128)S(1)} async-done(((s32[128,32,128]{2,1,0:T(8,128)}), s32[128,32,128]{2,1,0:T(8,128)S(1)}, u32[]{:S(2)}, u32[]{:S(2)}) %all-to-all-start.1) | async-done | bytes 2097184 | tf_op jit(solution)/shard_map/send_first/all_to_all | solution.py:460
  75.9 0.0 copy-start
  75.9 5.8 %all-to-all-start.2 = ((s32[128,24,128]{2,1,0:T(8,128)}), s32[128,24,128]{2,1,0:T(8,128)}, u32[]{:S(2)}, u32[]{:S(2)}) async-start(s32[128,24,128]{2,1,0:T(8,128)} %get-tuple-element.10), calls=%async_computation.2 | async-start | bytes 3145728 | tf_op jit(solution)/shard_map/send_rest/all_to_all | solution.py:460
  81.7 0.0 copy-done
  81.7 23.5 %batch_density_0.1 = (f32[2,4096]{1,0:T(2,128)}, f32[2,128]{1,0:T(2,128)}) custom-call(s32[32]{0:T(128)} %batch_tables.1.refs_0_, s32[128,32,128]{2,1,0:T(8,128)} %copy-done, s32[128,32,128]{2,1,0:T(8,128)} %copy-done, s32[128,32,128]{2,1,0:T(8,128)} %copy-done, s32[128,32,128]{2,1,0:T(8,128)} %copy-done, f32[8,128]{1,0:T(8,128)} %get-tuple-element.11.refs_5_, ...), custom_call_target="tpu_custom_call" | custom-call | flops 25999998976 | bytes 10000000 | tf_op jit(solution)/shard_map/batch_density_0/pallas_call | solution.py:412
  105.2 0.7 all-to-all-done.2
  105.9 21.5 %batch_density_1.1 = (f32[2,2,4096]{2,1,0:T(2,128)}, f32[128,2,128]{2,1,0:T(2,128)}) custom-call(s32[32]{0:T(128)} %batch_tables.1.refs_0_, s32[128,32,128]{2,1,0:T(8,128)} %copy-done, s32[3072,128]{1,0:T(8,128)} %bitcast.2.refs_2_, f32[2,128]{1,0:T(2,128)} %get-tuple-element.12.refs_3_, f32[2,4096]{1,0:T(2,128)} %get-tuple-element.13.refs_4_, ...), custom_call_target="tpu_custom_call" | custom-call | flops 25999998976 | bytes 10000000 | tf_op jit(solution)/shard_map/batch_density_1/pallas_call | solution.py:412
  127.3 19.0 %all_to_all.21 = f32[128,2,128]{2,1,0:T(2,128)} all-to-all(f32[128,2,128]{2,1,0:T(2,128)} %get-tuple-element.15), channel_id=1, replica_groups=mesh['row_0'=4,'row_1'=4,'col_0'=4,'col_1'=2] {'row_0','row_1','col_0','..., dimensions={0} | all-to-all | bytes 262144 | tf_op jit(solution)/shard_map/all_to_all | solution.py:460
  146.3 1.9 %moment_table.1 = f32[9,2,1024]{2,1,0:T(2,128)} custom-call(f32[256,128]{1,0:T(8,128)} %bitcast.22), custom_call_target="tpu_custom_call" | custom-call | tf_op jit(solution)/shard_map/moment_table/pallas_call | solution.py:450
Async XLA Ops:
  40.8 35.1 %all-to-all-start.1 = ((s32[128,32,128]{2,1,0:T(8,128)}), s32[128,32,128]{2,1,0:T(8,128)S(1)}, u32[]{:S(2)}, u32[]{:S(2)}) async-start(s32[128,32,128]{2,1,0:T(8,128)} %get-tuple-element.9), calls=%async_computation.1 | async-start | bytes 4194304 | tf_op jit(solution)/shard_map/send_first/all_to_all | solution.py:460
  75.9 5.8 %copy-start = (s32[128,32,128]{2,1,0:T(8,128)}, s32[128,32,128]{2,1,0:T(8,128)S(1)}, u32[]{:S(2)}) copy-start(s32[128,32,128]{2,1,0:T(8,128)S(1)} %all-to-all-done.1.refs_1_.refs_2_.refs_3_.refs_4_) | copy-start | bytes 6291460
  75.9 30.0 %all-to-all-start.2 = ((s32[128,24,128]{2,1,0:T(8,128)}), s32[128,24,128]{2,1,0:T(8,128)}, u32[]{:S(2)}, u32[]{:S(2)}) async-start(s32[128,24,128]{2,1,0:T(8,128)} %get-tuple-element.10), calls=%async_computation.2 | async-start | bytes 3145728 | tf_op jit(solution)/shard_map/send_rest/all_to_all | solution.py:460

commit v2 on v0

v2 whole, which is shorter than its diff:
```python
import jax
import jax.numpy as jnp
from jax import lax
from jax.experimental import pallas as pl
from jax.experimental.pallas import tpu as pltpu
from jax.sharding import Mesh
from jax.sharding import PartitionSpec as P

TILE = 128
KT = 7
NT = 96
PTS = 4096
ATOMS = 1024
N_ROW = 16
N_COL = 8
DEVICES = 128
SPAN = 12
ROW = ("row_0", "row_1")
COL = ("col_0", "col_1")
ROW_COL = ("row_0", "row_1", "col_0", "col_1")

SLOTS = 24
LINES = 32
PAIRS = KT * (KT + 1) // 2
WINDOW = 2 * PAIRS
FIRST = 32
REST = WINDOW - FIRST
SLOT_LINES = 24
FRONT = 1152
BACK = 1536
BLOCK = 1024
STEPS = PTS // BLOCK
ROUNDER = 12582912.0


def pair_start(last):
    return last * (last + 1) // 2


def spread_body(tile_list, tile_count, point_count, first, second, out, tiles, lines, sems):
    my_row = lax.axis_index(ROW)
    my_col = lax.axis_index(COL)
    own_start = [least_tile(tile_list, batch) for batch in slot_order(tile_count, point_count)]
    lead = lax.rem(my_col - my_row + 16, 8)
    base = (my_row - my_col + lead) // 8
    copies = []
    for half in range(2):
        for step in range(6):
            for which, stored in enumerate((first, second)):
                index = which * 12 + half * 6 + step
                column = jnp.clip(2 * step + base - half, 0, 11)
                copy = pltpu.make_async_copy(
                    stored.at[pl.ds(step * TILE, TILE), pl.ds(pl.multiple_of(column * TILE, TILE), TILE)],
                    tiles.at[index],
                    sems.at[index],
                )
                copy.start()
                copies.append((copy, index, half, step))
    largest = jnp.zeros((8, TILE), jnp.float32)
    for copy, index, half, step in copies:
        copy.wait()
        values = tiles[index].astype(jnp.float32)
        column = 2 * step + base - half
        shift = lead - 8 * half
        used = (column >= 0) & (column < 12) & (shift <= 6) & (shift >= -6)
        peak = jnp.max(jnp.abs(values).reshape(16, 8, TILE), axis=0)
        largest = jnp.maximum(largest, jnp.where(used, peak, 0.0))
        if half:
            values = values.T
        lines[pl.ds(index, TILE, stride=SLOTS), :] = values
    peak = jnp.max(largest)
    line = lax.broadcasted_iota(jnp.int32, (8, TILE), 0)
    extra = jnp.where(
        line == 0,
        own_start[0].astype(jnp.float32),
        jnp.where(line == 1, own_start[1].astype(jnp.float32), peak),
    )

    def pack(dest, carry):
        at = pl.multiple_of(dest * SLOTS, 8)
        low = lines[pl.ds(at, 16), :]
        high = lines[pl.ds(at + 16, 8), :]
        to = pl.multiple_of(dest * LINES, 16)
        out[pl.ds(to, 16), :] = low.astype(jnp.bfloat16)
        out[pl.ds(to + 16, 16), :] = jnp.concatenate([high, extra], axis=0).astype(jnp.bfloat16)
        return carry

    lax.fori_loop(0, DEVICES, pack, 0, unroll=4)


def spread(tile_list, tile_count, point_count, first, second):
    return pl.pallas_call(
        spread_body,
        out_shape=jax.ShapeDtypeStruct((DEVICES * LINES, TILE), jnp.bfloat16),
        in_specs=[
            pl.BlockSpec(memory_space=pltpu.SMEM),
            pl.BlockSpec(memory_space=pltpu.SMEM),
            pl.BlockSpec(memory_space=pltpu.SMEM),
            pl.BlockSpec(memory_space=pl.ANY),
            pl.BlockSpec(memory_space=pl.ANY),
        ],
        out_specs=pl.BlockSpec(memory_space=pltpu.VMEM),
        scratch_shapes=[
            pltpu.VMEM((SLOTS, TILE, TILE), jnp.bfloat16),
            pltpu.VMEM((DEVICES * SLOTS, TILE), jnp.float32),
            pltpu.SemaphoreType.DMA((SLOTS,)),
        ],
        name="spread_rows",
    )(tile_list, tile_count, point_count, first, second)


def window_body(arrived, out_first, out_rest, unit_out, lines, coded, start_lines, starts, sem):
    def widen(source, top):
        at = pl.multiple_of(source * LINES, 16)
        to = pl.multiple_of(FRONT + source * SLOTS, 8)
        low = arrived[pl.ds(at, 16), :].astype(jnp.float32)
        high = arrived[pl.ds(at + 16, 16), :].astype(jnp.float32)
        lines[pl.ds(to, 16), :] = low
        lines[pl.ds(to + 16, 8), :] = high[0:8]
        extra = high[8:16]
        peak, own = top
        lane = lax.broadcasted_iota(jnp.int32, (8, TILE), 1)
        own = jnp.where(lane == source, extra, own)
        return jnp.maximum(peak, extra), own

    zero = jnp.zeros((8, TILE), jnp.float32)
    tops, own = lax.fori_loop(0, DEVICES, widen, (zero, zero), unroll=4)
    start_lines[...] = own.astype(jnp.int32)
    copy = pltpu.make_async_copy(start_lines, starts, sem)
    copy.start()
    peak = jnp.broadcast_to(tops[2:3, :], (8, TILE))
    scale = jnp.full((8, TILE), 2.0**21, jnp.float32)
    unit = jnp.full((8, TILE), 2.0**-21, jnp.float32)
    for step in range(1, 64):
        small = peak < 2.0 ** (-7 - step)
        scale = jnp.where(small, 2.0 ** (21 + step), scale)
        unit = jnp.where(small, 2.0 ** (-21 - step), unit)
    unit_out[...] = unit

    order = lax.broadcasted_iota(jnp.int32, (8, TILE), 0)

    def line_of(row, col, which, half, step):
        return FRONT + (row * N_COL + col) * SLOTS + which * 12 + half * 6 + step

    def eight(start):
        return lines[pl.ds(start, 8, stride=(N_COL + 1) * SLOTS), :]

    for apart in range(KT):
        for group in range(NT // 8):
            words = []
            for which in range(2):
                odd = group % 2
                step = group // 2
                if odd or apart == 0:
                    total = eight(line_of(8 * odd - apart, 0, which, 0, step))
                else:
                    total = eight(line_of(-apart, 0, which, 0, step))
                    if step > 0:
                        before = eight(line_of(16 - apart, 0, which, 0, step - 1))
                        total = jnp.where(order < apart, before, total)
                if apart > 0:
                    after = eight(line_of(8 * odd, -apart, which, 1, step))
                    wrapped = eight(line_of(8 * odd, 8 - apart, which, 1, step))
                    total = total + jnp.where(order < apart, wrapped, after)
                total = total * scale
                words.append(((total + ROUNDER) - ROUNDER).astype(jnp.int32))
            word = (words[0] << 16) | (words[1] & 0xFFFF)
            coded[pl.ds(group * 64 + apart, 8, stride=8), :] = word

    copy.wait()

    def fill(dest, carry):
        for batch in range(2):
            begin = starts[batch, dest]
            for last in range(KT):
                words = coded[pl.ds(pl.multiple_of((begin + last) * 8, 8), 8), :]
                low = batch * PAIRS + pair_start(last)
                high = low + last + 1
                if low < FIRST:
                    cut = min(high, FIRST)
                    out_first[dest, low:cut, :] = words[0 : cut - low]
                if high > FIRST:
                    cut = max(low, FIRST)
                    out_rest[dest, cut - FIRST : high - FIRST, :] = words[cut - low : last + 1]
        return carry

    lax.fori_loop(0, DEVICES, fill, 0, unroll=2)


def windows(arrived):
    return pl.pallas_call(
        window_body,
        out_shape=(
            jax.ShapeDtypeStruct((DEVICES, FIRST, TILE), jnp.int32),
            jax.ShapeDtypeStruct((DEVICES, REST, TILE), jnp.int32),
            jax.ShapeDtypeStruct((8, TILE), jnp.float32),
        ),
        in_specs=[pl.BlockSpec(memory_space=pltpu.VMEM)],
        out_specs=tuple(pl.BlockSpec(memory_space=pltpu.VMEM) for _ in range(3)),
        scratch_shapes=[
            pltpu.VMEM((FRONT + DEVICES * SLOTS + BACK, TILE), jnp.float32),
            pltpu.VMEM((NT * 8, TILE), jnp.int32),
            pltpu.VMEM((8, TILE), jnp.int32),
            pltpu.SMEM((8, TILE), jnp.int32),
            pltpu.SemaphoreType.DMA,
        ],
        name="pick_windows",
    )(arrived)


def slot_order(tile_count, point_count):
    work = []
    for batch in range(2):
        count = tile_count[batch]
        passes = jnp.where(count >= KT, 28, jnp.where(count == KT - 1, 21, 15))
        work.append(passes * point_count[batch])
    swap = (work[1] > work[0]).astype(jnp.int32)
    return swap, 1 - swap


def least_tile(tile_list, batch):
    least = tile_list[batch, 0]
    for place in range(1, KT):
        least = jnp.minimum(least, tile_list[batch, place])
    return least


COUNT = 7
POINTS = 8
ATOM = 9
BATCH = 10
LINE = 11
ENTRIES = 40


def table_body(tile_list, tile_count, point_count, table, column_of, order_of):
    device = lax.axis_index(ROW) * N_COL + lax.axis_index(COL)
    for slot, batch in enumerate(slot_order(tile_count, point_count)):
        base = slot * ENTRIES
        start = least_tile(tile_list, batch)
        count = jnp.minimum(tile_count[batch], KT)
        for place in range(KT):
            column_of[tile_list[batch, place] - start] = place
        live_end = 0
        dead_end = count
        for rank in range(KT):
            place = column_of[rank]
            live = (place < count).astype(jnp.int32)
            to = jnp.where(live == 1, live_end, dead_end)
            table[base + to] = place
            order_of[to] = rank
            live_end = live_end + live
            dead_end = dead_end + 1 - live
        table[base + COUNT] = count
        table[base + POINTS] = point_count[batch]
        table[base + ATOM] = lax.rem((2 * device + batch) * 4, ATOMS)
        table[base + BATCH] = batch
        for last in range(KT):
            high = order_of[last]
            for first in range(last + 1):
                low = order_of[first]
                line = slot * (PAIRS - SLOT_LINES) + high * (high + 1) // 2 + high - low
                line = jnp.where(last < count, line, SLOT_LINES)
                table[base + LINE + pair_start(last) + first] = (line // 8) * (DEVICES * 8) + line % 8


def batch_tables(tile_list, tile_count, point_count):
    return pl.pallas_call(
        table_body,
        out_shape=jax.ShapeDtypeStruct((2 * ENTRIES,), jnp.int32),
        in_specs=[pl.BlockSpec(memory_space=pltpu.SMEM) for _ in range(3)],
        out_specs=pl.BlockSpec(memory_space=pltpu.SMEM),
        scratch_shapes=[pltpu.SMEM((8,), jnp.int32), pltpu.SMEM((8,), jnp.int32)],
        name="batch_tables",
    )(tile_list, tile_count, point_count)


def batch_body(slot, *refs):
    table_in, first_rows = refs[:2]
    refs = refs[2:]
    if slot:
        rest_rows, before_in, earlier_in = refs[:3]
        refs = refs[3:]
        sources = [first_rows.at[:, pl.ds(FIRST - 8, 8), :]]
        sources += [rest_rows.at[:, pl.ds(8 * group, 8), :] for group in range(REST // 8)]
    else:
        sources = [first_rows.at[:, pl.ds(8 * group, 8), :] for group in range(FIRST // 8)]
    unit_in, offsets_in, weights_in, atoms_in, basis, density_out, payload_out = refs[:7]
    (
        table, high_part, low_part, rows, values_in, density, payload,
        unit, offsets, weights, atoms, before, earlier, sums_kept,
        table_sem, row_sems, value_sems, side_sems, out_sems,
    ) = refs[7:]
    base = slot * ENTRIES

    table_copy = pltpu.make_async_copy(table_in, table, table_sem)
    table_copy.start()
    row_copies = [
        pltpu.make_async_copy(source, rows.at[group], row_sems.at[group])
        for group, source in enumerate(sources)
    ]
    for copy in row_copies:
        copy.start()
    pairs = [(unit_in, unit), (offsets_in, offsets), (weights_in, weights), (atoms_in, atoms)]
    if slot:
        pairs += [(before_in, before), (earlier_in, earlier)]
    side_copies = [
        pltpu.make_async_copy(source, target, side_sems.at[place])
        for place, (source, target) in enumerate(pairs)
    ]
    table_copy.wait()
    count = table[base + COUNT]
    live_points = table[base + POINTS]
    base_atom = table[base + ATOM]
    batch = table[base + BATCH]

    def value_copy(step):
        return pltpu.make_async_copy(
            basis.at[pl.ds(pl.multiple_of(batch * PTS + step * BLOCK, BLOCK), BLOCK), :],
            values_in.at[pl.ds(pl.multiple_of(step * BLOCK, BLOCK), BLOCK), :],
            value_sems.at[step],
        )

    for step in range(STEPS):
        pl.when(step * BLOCK < live_points)(lambda step=step: value_copy(step).start())
    for copy in side_copies:
        copy.start()
    if not slot:
        density[...] = jnp.zeros((2, PTS), jnp.float32)
    for copy in row_copies:
        copy.wait()
    lines = rows.reshape(len(sources) * DEVICES * 8, TILE)

    def unpack(last):
        for first in range(last + 1):
            start = table[base + LINE + pair_start(last) + first]
            words = lines[pl.ds(start, TILE, stride=8), :]
            down = slice(first * TILE, (first + 1) * TILE)
            for matrix in range(2):
                value = words >> 16 if matrix == 0 else (words << 16) >> 16
                value = value.astype(jnp.float32)
                top = value.astype(jnp.bfloat16)
                at = (2 * last + matrix) * TILE
                high_part[down, at : at + TILE] = top
                if first < last:
                    bottom = (value - top.astype(jnp.float32)).astype(jnp.bfloat16)
                    low_part[down, at : at + TILE] = bottom

    for last in range(KT - 2):
        unpack(last)
    for last in range(KT - 2, KT):
        pl.when(count > last)(lambda last=last: unpack(last))
    for copy in side_copies:
        copy.wait()
    if slot:
        which = lax.broadcasted_iota(jnp.int32, (2, PTS), 0)
        for matrix in range(2):
            other = jnp.broadcast_to(earlier[matrix : matrix + 1, :], (2, PTS))
            density[matrix] = jnp.where(which == batch, 0.0, other)

    blocks = (live_points + BLOCK - 1) // BLOCK

    def reduce(step):
        start = pl.multiple_of(step * BLOCK, BLOCK)
        point = start + lax.broadcasted_iota(jnp.int32, (1, BLOCK), 1)
        scale = jnp.where(point < live_points, unit[0:1, 0:1], 0.0)
        at = pl.ds(start, BLOCK)
        for matrix in range(2):
            pieces = [
                jnp.sum(sums_kept[matrix, cut : cut + TILE, :].T, axis=0, keepdims=True)
                for cut in range(0, BLOCK, TILE)
            ]
            line = jnp.concatenate(pieces, axis=1) * scale
            if slot:
                density[matrix, pl.ds(batch, 1), at] = line
            else:
                density[matrix : matrix + 1, at] = line

    def densities(tiles):
        def block(step, carry):
            value_copy(step).wait()
            reduce(jnp.maximum(step - 1, 0))
            start = pl.multiple_of(step * BLOCK, BLOCK)
            columns = []
            for place in range(tiles):
                lane = pl.multiple_of(table[base + place] * TILE, TILE)
                columns.append(values_in[pl.ds(start, BLOCK), pl.ds(lane, TILE)])
            values = jnp.concatenate(columns, axis=1)
            sums = [None, None]
            for last in range(tiles):
                cols = slice(2 * last * TILE, (2 * last + 2) * TILE)
                down = (last + 1) * TILE
                got = jnp.dot(
                    values[:, :down], high_part[:down, cols], preferred_element_type=jnp.float32
                )
                if last:
                    down = last * TILE
                    got = got + jnp.dot(
                        values[:, :down], low_part[:down, cols], preferred_element_type=jnp.float32
                    )
                column = columns[last].astype(jnp.float32)
                for matrix in range(2):
                    part = got[:, matrix * TILE : (matrix + 1) * TILE] * column
                    sums[matrix] = part if last == 0 else sums[matrix] + part
            for matrix in range(2):
                sums_kept[matrix] = sums[matrix]
            return carry

        lax.fori_loop(0, blocks, block, 0)

    for tiles in range(KT - 2, KT + 1):
        pl.when(count == tiles)(lambda tiles=tiles: densities(tiles))
    reduce(jnp.maximum(blocks - 1, 0))

    density_copy = pltpu.make_async_copy(density, density_out, out_sems.at[0])
    density_copy.start()
    mine = pl.ds(batch, 1)
    x = offsets[0, mine, :]
    y = offsets[1, mine, :]
    z = offsets[2, mine, :]
    weight = weights[mine, :]
    near = lax.rem(atoms[mine, :] - base_atom + 2 * ATOMS, ATOMS)
    squared = x * x + y * y + z * z
    shapes = [
        jnp.ones_like(x), x, y, z, x * y, y * z,
        3.0 * z * z - squared, x * z, x * x - y * y,
    ]
    shapes = jnp.concatenate([weight * shape for shape in shapes], axis=0)
    lane = lax.broadcasted_iota(jnp.int32, (9, TILE), 1)
    degree = lax.broadcasted_iota(jnp.int32, (9, TILE), 0)
    lane = lane - degree * SPAN - 4 * batch
    for matrix in range(2):
        terms = density[matrix, mine, :] if slot else density[matrix : matrix + 1, :]
        terms = terms * shapes
        total = jnp.zeros((9, TILE), jnp.float32)
        for atom in range(8):
            picked = jnp.sum(jnp.where(near == atom, terms, 0.0), axis=1, keepdims=True)
            total = total + jnp.where(lane == atom, picked, 0.0)
        line = jnp.sum(total, axis=0, keepdims=True)
        if slot:
            line = line + before[matrix : matrix + 1, :]
            payload[:, matrix : matrix + 1, :] = jnp.broadcast_to(line[None], (DEVICES, 1, TILE))
        else:
            payload[matrix : matrix + 1, :] = line
    payload_copy = pltpu.make_async_copy(payload, payload_out, out_sems.at[1])
    payload_copy.start()
    payload_copy.wait()
    density_copy.wait()


def batch_call(slot, table, rows, carried, unit, offsets, weights, atoms, basis):
    arrays = [table, *rows, *carried, unit, offsets, weights, atoms, basis]
    payload = (DEVICES, 2, TILE) if slot else (2, TILE)
    density = (2, 2, PTS) if slot else (2, PTS)

    def body(*refs):
        batch_body(slot, *refs)

    return pl.pallas_call(
        body,
        in_specs=[pl.BlockSpec(memory_space=pl.ANY) for _ in arrays],
        out_specs=(pl.BlockSpec(memory_space=pl.ANY), pl.BlockSpec(memory_space=pl.ANY)),
        out_shape=(
            jax.ShapeDtypeStruct(density, jnp.float32),
            jax.ShapeDtypeStruct(payload, jnp.float32),
        ),
        scratch_shapes=[
            pltpu.SMEM((2 * ENTRIES,), jnp.int32),
            pltpu.VMEM((KT * TILE, 2 * KT * TILE), jnp.bfloat16),
            pltpu.VMEM(((KT - 1) * TILE, 2 * KT * TILE), jnp.bfloat16),
            pltpu.VMEM((4, DEVICES, 8, TILE), jnp.int32),
            pltpu.VMEM((PTS, KT * TILE), jnp.bfloat16),
            pltpu.VMEM(density, jnp.float32),
            pltpu.VMEM(payload, jnp.float32),
            pltpu.VMEM((8, TILE), jnp.float32),
            pltpu.VMEM((3, 2, PTS), jnp.float32),
            pltpu.VMEM((2, PTS), jnp.float32),
            pltpu.VMEM((2, PTS), jnp.int32),
            pltpu.VMEM((2, TILE), jnp.float32),
            pltpu.VMEM((2, PTS), jnp.float32),
            pltpu.VMEM((2, BLOCK, TILE), jnp.float32),
            pltpu.SemaphoreType.DMA,
            pltpu.SemaphoreType.DMA((4,)),
            pltpu.SemaphoreType.DMA((STEPS,)),
            pltpu.SemaphoreType.DMA((6,)),
            pltpu.SemaphoreType.DMA((2,)),
        ],
        compiler_params=pltpu.CompilerParams(vmem_limit_bytes=60 * 1024 * 1024),
        cost_estimate=pl.CostEstimate(
            flops=26_000_000_000, bytes_accessed=10_000_000, transcendentals=0
        ),
        name=f"batch_density_{slot}",
    )(*arrays)


def moment_body(arrived, out):
    lane = lax.broadcasted_iota(jnp.int32, (8, TILE), 1)
    for matrix in range(2):
        totals = [jnp.zeros((8, TILE), jnp.float32) for _ in range(9)]
        for place in range(16):
            part = arrived[pl.ds(2 * place + matrix, 8, stride=32), :]
            for degree in range(9):
                moved = pltpu.roll(part, (8 * place - SPAN * degree) % TILE, 1)
                if place < 15:
                    mine = (lane >= 8 * place) & (lane < 8 * place + SPAN)
                    totals[degree] = totals[degree] + jnp.where(mine, moved, 0.0)
                else:
                    inside = jnp.where(lane >= 8 * place, moved, 0.0)
                    after = pltpu.roll(jnp.where(lane < SPAN - 8, moved, 0.0), 1, 0)
                    totals[degree] = totals[degree] + inside + after
        for degree in range(9):
            for block in range(8):
                out[degree, matrix : matrix + 1, block * TILE : (block + 1) * TILE] = totals[degree][
                    block : block + 1, :
                ]


def moment_table(arrived):
    return pl.pallas_call(
        moment_body,
        out_shape=jax.ShapeDtypeStruct((9, 2, ATOMS), jnp.float32),
        in_specs=[pl.BlockSpec(memory_space=pltpu.VMEM)],
        out_specs=pl.BlockSpec(memory_space=pltpu.VMEM),
        name="moment_table",
    )(arrived)


def exchange(value):
    return lax.all_to_all(value, ROW_COL, 0, 0, tiled=True)


def local(
    density_first,
    density_second,
    basis,
    tile_list,
    tile_count,
    point_count,
    offsets,
    weights,
    atom_of_point,
):
    rows = spread(tile_list, tile_count, point_count, density_first, density_second)
    rows = exchange(rows.reshape(DEVICES, LINES, TILE)).reshape(DEVICES * LINES, TILE)
    first, rest, unit = windows(rows)
    with jax.named_scope("send_first"):
        first = exchange(first)
    with jax.named_scope("send_rest"):
        rest = exchange(rest)

    table = batch_tables(tile_list, tile_count, point_count)
    flat = basis.reshape(-1, KT * TILE)
    side = (unit, offsets, weights, atom_of_point)
    density_0, payload_0 = batch_call(0, table, (first,), (), *side, flat)
    density, payload = batch_call(
        1, table, (first, rest), (payload_0, density_0), *side, flat
    )
    moments = moment_table(exchange(payload).reshape(DEVICES * 2, TILE)).swapaxes(0, 1)
    return density, moments


def solution(mesh):
    torus = Mesh(mesh.devices.reshape(4, 4, 4, 2), ("row_0", "row_1", "col_0", "col_1"))
    in_specs = (
        P(ROW, COL),
        P(ROW, COL),
        P(ROW_COL, None, None),
        P(ROW_COL, None),
        P(ROW_COL),
        P(ROW_COL),
        P(None, ROW_COL, None),
        P(ROW_COL, None),
        P(ROW_COL, None),
    )
    out_specs = (P(None, ROW_COL, None), P())
    return jax.shard_map(local, mesh=torus, in_specs=in_specs, out_specs=out_specs, check_vma=False)
```

time: 162 us -> 144 us (0.89); the launches traced: 161 us -> 141 us
  blocking collectives: 30.4 us -> 50.7 us
  starting transfers between devices: 27.1 us -> 10.6 us
  Pallas kernels: 57.1 us -> 44.3 us
  local copies, waits for them, and re-layouts: 4.47 us -> 0.01 us
  other arithmetic: 3.9 us -> 0 us
  waiting for transfers between devices: 37.6 us -> 34.9 us
    all_to_all x1 -> x2, blocking collectives: 30.4 us -> 50.7 us  [exchange(): return lax.all_to_all(value, ROW_COL, 0, 0, tiled=True)]
    all_to_all x3 -> x2, starting transfers between devices: 27.1 us -> 10.6 us  [exchange(): return lax.all_to_all(value, ROW_COL, 0, 0, tiled=True)]
    pallas_call x3 -> x4, Pallas kernels: 47.3 us -> 34.5 us  [the longest x2 30.8 us: batch_call(): pl.pallas_call(body, in_specs=[pl.BlockSpec(memory_space=pl.ANY) for _ in...]
    unnamed x18 -> x2, local copies, waits for them, and re-layouts: 2.96 us -> 0.01 us
    all_to_all x3 -> x2, waiting for transfers between devices: 37.6 us -> 34.9 us  [exchange(): return lax.all_to_all(value, ROW_COL, 0, 0, tiled=True)]
  transfers between devices with their start and end apart: 3 -> 2, of which waited for: 3 -> 2; matrix products, arithmetic and copies ran while one was open for 2% -> 0% of each run, Pallas kernels for 15% -> 14%
where the time goes in v2:
time: 144 us; the launch traced here: 141 us
  blocking collectives  50.7 us (35%)
  Pallas kernels  44.3 us (31%)
  waiting for transfers between devices  34.9 us (24%)
  starting transfers between devices  10.6 us (7%)
    all_to_all x2, blocking collectives, exchange(): return lax.all_to_all(value, ROW_COL, 0, 0, tiled=True)  50.7 us
    all_to_all x2, waiting for transfers between devices, exchange(): return lax.all_to_all(value, ROW_COL, 0, 0, tiled=True)  34.9 us
    pallas_call x2, Pallas kernels, batch_call(): pl.pallas_call(body, in_specs=[pl.BlockSpec(memory_space=pl.ANY) for _ in...  30.8 us
    all_to_all x2, starting transfers between devices, exchange(): return lax.all_to_all(value, ROW_COL, 0, 0, tiled=True)  10.6 us
    pallas_call x1, Pallas kernels, windows(): pl.pallas_call(window_body, out_shape=(jax.ShapeDtypeStruct((DEVICES, FIR...  5.19 us
    pallas_call x1, Pallas kernels, spread(): pl.pallas_call(spread_body, out_shape=jax.ShapeDtypeStruct((DEVICES * LIN...  4.64 us
  transfers between devices with their start and end apart: 2, of which 2 were waited for; matrix products, arithmetic and copies ran while one was open for 0% of the time, Pallas kernels for 14%

profile of v2, /device:TPU:1, one launch (start us, length us, event | category | flops | bytes accessed | tf_op | source)
XLA Modules:
  0.0 141.3 jit_solution(968223535686511479)
XLA Ops:
  0.6 4.6 %spread_rows.1 = bf16[4096,128]{1,0:T(8,128)(2,1)} custom-call(s32[2,7]{1,0:T(2,128)} %tile_list.3, s32[2]{0:T(128)} %tile_count.3, s32[2]{0:T(128)} %point_count.3, bf16[768,1536]{1,0:T(8,128)(2,1)} %first.1, bf16[768,1536]{1,0:T(8,128)(2,1)} %second.1), custom_call_target="tpu_custom_call" | custom-call | tf_op jit(solution)/shard_map/spread_rows/pallas_call | solution.py:92
  5.3 30.4 %all_to_all.20 = bf16[128,32,128]{2,1,0:T(8,128)(2,1)} all-to-all(bf16[128,32,128]{2,1,0:T(8,128)(2,1)} %bitcast.6), channel_id=1, replica_groups=mesh['row_0'=4,'row_1'=4,'col_0'=4,'col_1'=2] {'row_0','row_1','col_0','..., dimensions={0} | all-to-all | bytes 2097152 | tf_op jit(solution)/shard_map/all_to_all | solution.py:529
  35.7 5.2 %pick_windows.1 = (s32[128,32,128]{2,1,0:T(8,128)}, s32[128,24,128]{2,1,0:T(8,128)}, f32[8,128]{1,0:T(8,128)}) custom-call(bf16[4096,128]{1,0:T(8,128)(2,1)} %bitcast.5), custom_call_target="tpu_custom_call" | custom-call | tf_op jit(solution)/shard_map/pick_windows/pallas_call | solution.py:191
  40.9 4.8 %all-to-all-start.1 = ((s32[128,32,128]{2,1,0:T(8,128)}), s32[128,32,128]{2,1,0:T(8,128)S(1)}, u32[]{:S(2)}, u32[]{:S(2)}) async-start(s32[128,32,128]{2,1,0:T(8,128)} %get-tuple-element.9), calls=%async_computation.1 | async-start | bytes 4194304 | tf_op jit(solution)/shard_map/send_first/all_to_all | solution.py:529
  45.7 1.8 %batch_tables.1.refs_0_ = s32[80]{0:T(128)} custom-call(s32[2,7]{1,0:T(2,128)} %tile_list.3, s32[2]{0:T(128)} %tile_count.3, s32[2]{0:T(128)} %point_count.3), custom_call_target="tpu_custom_call" | custom-call | tf_op jit(solution)/shard_map/batch_tables/pallas_call | solution.py:268
  47.5 28.5 %all-to-all-done.1.refs_1_ = s32[128,32,128]{2,1,0:T(8,128)S(1)} async-done(((s32[128,32,128]{2,1,0:T(8,128)}), s32[128,32,128]{2,1,0:T(8,128)S(1)}, u32[]{:S(2)}, u32[]{:S(2)}) %all-to-all-start.1) | async-done | bytes 2097184 | tf_op jit(solution)/shard_map/send_first/all_to_all | solution.py:529
  75.9 0.0 copy-start
  75.9 5.8 %all-to-all-start.2 = ((s32[128,24,128]{2,1,0:T(8,128)}), s32[128,24,128]{2,1,0:T(8,128)}, u32[]{:S(2)}, u32[]{:S(2)}) async-start(s32[128,24,128]{2,1,0:T(8,128)} %get-tuple-element.10), calls=%async_computation.2 | async-start | bytes 3145728 | tf_op jit(solution)/shard_map/send_rest/all_to_all | solution.py:529
  81.7 0.0 copy-done
  81.7 17.7 %batch_density_0.1 = (f32[2,4096]{1,0:T(2,128)}, f32[2,128]{1,0:T(2,128)}) custom-call(s32[80]{0:T(128)} %batch_tables.1.refs_0_, s32[128,32,128]{2,1,0:T(8,128)} %copy-done, f32[8,128]{1,0:T(8,128)} %get-tuple-element.11.refs_2_.refs_5_, f32[3,2,4096]{2,1,0:T(2,128)} %refs_6_.1, f32[2,4096]{1,0:T(2,128)} %refs_7_.1, s32[2,4096]{1,0:T(2,128)} %refs_8_.1, ...), custom_call_target="tpu_custom_call" | custom-call | flops 25999998976 | bytes 10000000 | tf_op jit(solution)/shard_map/batch_density_0/pallas_call | solution.py:459
  99.4 6.5 %all-to-all-done.2.refs_2_ = s32[128,24,128]{2,1,0:T(8,128)} async-done(((s32[128,24,128]{2,1,0:T(8,128)}), s32[128,24,128]{2,1,0:T(8,128)}, u32[]{:S(2)}, u32[]{:S(2)}) %all-to-all-start.2) | async-done | bytes 1572896 | tf_op jit(solution)/shard_map/send_rest/all_to_all | solution.py:529
  105.9 13.1 %batch_density_1.1 = (f32[2,2,4096]{2,1,0:T(2,128)}, f32[128,2,128]{2,1,0:T(2,128)}) custom-call(s32[80]{0:T(128)} %batch_tables.1.refs_0_, s32[128,32,128]{2,1,0:T(8,128)} %copy-done, s32[128,24,128]{2,1,0:T(8,128)} %all-to-all-done.2.refs_2_, f32[2,128]{1,0:T(2,128)} %get-tuple-element.12.refs_3_, f32[2,4096]{1,0:T(2,128)} %get-tuple-element.13.refs_4_, ...), custom_call_target="tpu_custom_call" | custom-call | flops 25999998976 | bytes 10000000 | tf_op jit(solution)/shard_map/batch_density_1/pallas_call | solution.py:459
  119.0 20.3 %all_to_all.21 = f32[128,2,128]{2,1,0:T(2,128)} all-to-all(f32[128,2,128]{2,1,0:T(2,128)} %get-tuple-element.15), channel_id=1, replica_groups=mesh['row_0'=4,'row_1'=4,'col_0'=4,'col_1'=2] {'row_0','row_1','col_0','..., dimensions={0} | all-to-all | bytes 262144 | tf_op jit(solution)/shard_map/all_to_all | solution.py:529
  139.3 1.9 %moment_table.1 = f32[9,2,1024]{2,1,0:T(2,128)} custom-call(f32[256,128]{1,0:T(8,128)} %bitcast.7), custom_call_target="tpu_custom_call" | custom-call | tf_op jit(solution)/shard_map/moment_table/pallas_call | solution.py:519
Async XLA Ops:
  40.9 35.1 %all-to-all-start.1 = ((s32[128,32,128]{2,1,0:T(8,128)}), s32[128,32,128]{2,1,0:T(8,128)S(1)}, u32[]{:S(2)}, u32[]{:S(2)}) async-start(s32[128,32,128]{2,1,0:T(8,128)} %get-tuple-element.9), calls=%async_computation.1 | async-start | bytes 4194304 | tf_op jit(solution)/shard_map/send_first/all_to_all | solution.py:529
  75.9 5.8 %copy-start = (s32[128,32,128]{2,1,0:T(8,128)}, s32[128,32,128]{2,1,0:T(8,128)S(1)}, u32[]{:S(2)}) copy-start(s32[128,32,128]{2,1,0:T(8,128)S(1)} %all-to-all-done.1.refs_1_) | copy-start | bytes 6291460
  75.9 30.0 %all-to-all-start.2 = ((s32[128,24,128]{2,1,0:T(8,128)}), s32[128,24,128]{2,1,0:T(8,128)}, u32[]{:S(2)}, u32[]{:S(2)}) async-start(s32[128,24,128]{2,1,0:T(8,128)} %get-tuple-element.10), calls=%async_computation.2 | async-start | bytes 3145728 | tf_op jit(solution)/shard_map/send_rest/all_to_all | solution.py:529

commit v3 on v2

--- a/solution.py
+++ b/solution.py
@@ -25,10 +25,11 @@
 WINDOW = 2 * PAIRS
 FIRST = 32
 REST = WINDOW - FIRST
+GROUPS = 4
 SLOT_LINES = 24
 FRONT = 1152
 BACK = 1536
-BLOCK = 1024
+BLOCK = 512
 STEPS = PTS // BLOCK
 ROUNDER = 12582912.0
 
@@ -37,10 +38,20 @@
     return last * (last + 1) // 2
 
 
-def spread_body(tile_list, tile_count, point_count, first, second, out, tiles, lines, sems):
+def spread_body(
+    list_in, tiles_in, points_in, first, second, out,
+    tiles, lines, tile_list, tile_count, point_count, sems,
+):
     my_row = lax.axis_index(ROW)
     my_col = lax.axis_index(COL)
-    own_start = [least_tile(tile_list, batch) for batch in slot_order(tile_count, point_count)]
+    small = [
+        pltpu.make_async_copy(source, target, sems.at[SLOTS + place])
+        for place, (source, target) in enumerate(
+            ((list_in, tile_list), (tiles_in, tile_count), (points_in, point_count))
+        )
+    ]
+    for copy in small:
+        copy.start()
     lead = lax.rem(my_col - my_row + 16, 8)
     base = (my_row - my_col + lead) // 8
     copies = []
@@ -68,6 +79,9 @@
         if half:
             values = values.T
         lines[pl.ds(index, TILE, stride=SLOTS), :] = values
+    for copy in small:
+        copy.wait()
+    own_start = [least_tile(tile_list, batch) for batch in slot_order(tile_count, point_count)]
     peak = jnp.max(largest)
     line = lax.broadcasted_iota(jnp.int32, (8, TILE), 0)
     extra = jnp.where(
@@ -91,11 +105,11 @@
 def spread(tile_list, tile_count, point_count, first, second):
     return pl.pallas_call(
         spread_body,
-        out_shape=jax.ShapeDtypeStruct((DEVICES * LINES, TILE), jnp.bfloat16),
+        out_shape=pltpu.VMEM((DEVICES * LINES, TILE), jnp.bfloat16),
         in_specs=[
-            pl.BlockSpec(memory_space=pltpu.SMEM),
-            pl.BlockSpec(memory_space=pltpu.SMEM),
-            pl.BlockSpec(memory_space=pltpu.SMEM),
+            pl.BlockSpec(memory_space=pl.ANY),
+            pl.BlockSpec(memory_space=pl.ANY),
+            pl.BlockSpec(memory_space=pl.ANY),
             pl.BlockSpec(memory_space=pl.ANY),
             pl.BlockSpec(memory_space=pl.ANY),
         ],
@@ -103,13 +117,19 @@
         scratch_shapes=[
             pltpu.VMEM((SLOTS, TILE, TILE), jnp.bfloat16),
             pltpu.VMEM((DEVICES * SLOTS, TILE), jnp.float32),
-            pltpu.SemaphoreType.DMA((SLOTS,)),
+            pltpu.SMEM((2, KT), jnp.int32),
+            pltpu.SMEM((2,), jnp.int32),
+            pltpu.SMEM((2,), jnp.int32),
+            pltpu.SemaphoreType.DMA((SLOTS + 3,)),
         ],
         name="spread_rows",
     )(tile_list, tile_count, point_count, first, second)
 
 
-def window_body(arrived, out_first, out_rest, unit_out, lines, coded, start_lines, starts, sem):
+def window_body(
+    arrived, first_out, coded_to, starts_to, unit_to,
+    lines, coded, start_lines, starts, out_first, unit_out, sem, out_sems,
+):
     def widen(source, top):
         at = pl.multiple_of(source * LINES, 16)
         to = pl.multiple_of(FRONT + source * SLOTS, 8)
@@ -128,6 +148,8 @@
     start_lines[...] = own.astype(jnp.int32)
     copy = pltpu.make_async_copy(start_lines, starts, sem)
     copy.start()
+    starts_copy = pltpu.make_async_copy(start_lines, starts_to, out_sems.at[2])
+    starts_copy.start()
     peak = jnp.broadcast_to(tops[2:3, :], (8, TILE))
     scale = jnp.full((8, TILE), 2.0**21, jnp.float32)
     unit = jnp.full((8, TILE), 2.0**-21, jnp.float32)
@@ -136,6 +158,8 @@
         scale = jnp.where(small, 2.0 ** (21 + step), scale)
         unit = jnp.where(small, 2.0 ** (-21 - step), unit)
     unit_out[...] = unit
+    unit_copy = pltpu.make_async_copy(unit_out, unit_to, out_sems.at[0])
+    unit_copy.start()
 
     order = lax.broadcasted_iota(jnp.int32, (8, TILE), 0)
 
@@ -167,45 +191,85 @@
             word = (words[0] << 16) | (words[1] & 0xFFFF)
             coded[pl.ds(group * 64 + apart, 8, stride=8), :] = word
 
+    coded_copy = pltpu.make_async_copy(coded, coded_to, out_sems.at[1])
+    coded_copy.start()
     copy.wait()
-
+    copies = fill_windows(starts, coded, out_first, first_out, 0, FIRST, out_sems)
+    for copy in [unit_copy, starts_copy, coded_copy, *copies]:
+        copy.wait()
+
+
+def fill_windows(starts, coded, filled, out, begin, end, sems):
     def fill(dest, carry):
-        for batch in range(2):
-            begin = starts[batch, dest]
+        for slot in range(2):
+            start = starts[slot, dest]
             for last in range(KT):
-                words = coded[pl.ds(pl.multiple_of((begin + last) * 8, 8), 8), :]
-                low = batch * PAIRS + pair_start(last)
+                low = slot * PAIRS + pair_start(last)
                 high = low + last + 1
-                if low < FIRST:
-                    cut = min(high, FIRST)
-                    out_first[dest, low:cut, :] = words[0 : cut - low]
-                if high > FIRST:
-                    cut = max(low, FIRST)
-                    out_rest[dest, cut - FIRST : high - FIRST, :] = words[cut - low : last + 1]
+                top = max(low, begin)
+                bottom = min(high, end)
+                if top < bottom:
+                    words = coded[pl.ds(pl.multiple_of((start + last) * 8, 8), 8), :]
+                    filled[dest, top - begin : bottom - begin, :] = words[top - low : bottom - low]
         return carry
 
-    lax.fori_loop(0, DEVICES, fill, 0, unroll=2)
+    copies = []
+    group = DEVICES // GROUPS
+    for part in range(GROUPS):
+        lax.fori_loop(part * group, (part + 1) * group, fill, 0, unroll=2)
+        span = pl.ds(part * group, group)
+        copy = pltpu.make_async_copy(filled.at[span], out.at[span], sems.at[3 + part])
+        copy.start()
+        copies.append(copy)
+    return copies
 
 
 def windows(arrived):
     return pl.pallas_call(
         window_body,
         out_shape=(
-            jax.ShapeDtypeStruct((DEVICES, FIRST, TILE), jnp.int32),
-            jax.ShapeDtypeStruct((DEVICES, REST, TILE), jnp.int32),
-            jax.ShapeDtypeStruct((8, TILE), jnp.float32),
+            pltpu.HBM((DEVICES, FIRST, TILE), jnp.int32),
+            pltpu.HBM((NT * 8, TILE), jnp.int32),
+            pltpu.HBM((8, TILE), jnp.int32),
+            pltpu.HBM((8, TILE), jnp.float32),
         ),
         in_specs=[pl.BlockSpec(memory_space=pltpu.VMEM)],
-        out_specs=tuple(pl.BlockSpec(memory_space=pltpu.VMEM) for _ in range(3)),
+        out_specs=tuple(pl.BlockSpec(memory_space=pl.ANY) for _ in range(4)),
         scratch_shapes=[
             pltpu.VMEM((FRONT + DEVICES * SLOTS + BACK, TILE), jnp.float32),
             pltpu.VMEM((NT * 8, TILE), jnp.int32),
             pltpu.VMEM((8, TILE), jnp.int32),
             pltpu.SMEM((8, TILE), jnp.int32),
+            pltpu.VMEM((DEVICES, FIRST, TILE), jnp.int32),
+            pltpu.VMEM((8, TILE), jnp.float32),
             pltpu.SemaphoreType.DMA,
+            pltpu.SemaphoreType.DMA((3 + GROUPS,)),
         ],
+        compiler_params=pltpu.CompilerParams(vmem_limit_bytes=24 * 1024 * 1024),
         name="pick_windows",
     )(arrived)
+
+
+def rest_body(starts, coded, out, filled, sems):
+    for copy in fill_windows(starts, coded, filled, out, FIRST, WINDOW, sems):
+        copy.wait()
+
+
+def rest_windows(starts, coded):
+    return pl.pallas_call(
+        rest_body,
+        out_shape=jax.ShapeDtypeStruct((DEVICES, REST, TILE), jnp.int32),
+        in_specs=[
+            pl.BlockSpec(memory_space=pltpu.SMEM),
+            pl.BlockSpec(memory_space=pltpu.VMEM),
+        ],
+        out_specs=pl.BlockSpec(memory_space=pl.ANY),
+        scratch_shapes=[
+            pltpu.VMEM((DEVICES, REST, TILE), jnp.int32),
+            pltpu.SemaphoreType.DMA((3 + GROUPS,)),
+        ],
+        name="pick_rest",
+    )(starts, coded)
 
 
 def slot_order(tile_count, point_count):
@@ -287,11 +351,13 @@
         sources = [first_rows.at[:, pl.ds(8 * group, 8), :] for group in range(FIRST // 8)]
     unit_in, offsets_in, weights_in, atoms_in, basis, density_out, payload_out = refs[:7]
     (
-        table, high_part, low_part, rows, values_in, density, payload,
+        table, parts, rows, values_in, density, payload,
         unit, offsets, weights, atoms, before, earlier, sums_kept,
         table_sem, row_sems, value_sems, side_sems, out_sems,
     ) = refs[7:]
     base = slot * ENTRIES
+    if slot:
+        payload = payload_out
 
     table_copy = pltpu.make_async_copy(table_in, table, table_sem)
     table_copy.start()
@@ -341,10 +407,10 @@
                 value = value.astype(jnp.float32)
                 top = value.astype(jnp.bfloat16)
                 at = (2 * last + matrix) * TILE
-                high_part[down, at : at + TILE] = top
+                parts[down, at : at + TILE] = top
                 if first < last:
                     bottom = (value - top.astype(jnp.float32)).astype(jnp.bfloat16)
-                    low_part[down, at : at + TILE] = bottom
+                    parts[(last + 1 + first) * TILE : (last + 2 + first) * TILE, at : at + TILE] = bottom
 
     for last in range(KT - 2):
         unpack(last)
@@ -390,14 +456,10 @@
             for last in range(tiles):
                 cols = slice(2 * last * TILE, (2 * last + 2) * TILE)
                 down = (last + 1) * TILE
+                both = jnp.concatenate(columns[: last + 1] + columns[:last], axis=1)
                 got = jnp.dot(
-                    values[:, :down], high_part[:down, cols], preferred_element_type=jnp.float32
+                    both, parts[: (2 * last + 1) * TILE, cols], preferred_element_type=jnp.float32
                 )
-                if last:
-                    down = last * TILE
-                    got = got + jnp.dot(
-                        values[:, :down], low_part[:down, cols], preferred_element_type=jnp.float32
-                    )
                 column = columns[last].astype(jnp.float32)
                 for matrix in range(2):
                     part = got[:, matrix * TILE : (matrix + 1) * TILE] * column
@@ -442,9 +504,10 @@
             payload[:, matrix : matrix + 1, :] = jnp.broadcast_to(line[None], (DEVICES, 1, TILE))
         else:
             payload[matrix : matrix + 1, :] = line
-    payload_copy = pltpu.make_async_copy(payload, payload_out, out_sems.at[1])
-    payload_copy.start()
-    payload_copy.wait()
+    if not slot:
+        payload_copy = pltpu.make_async_copy(payload, payload_out, out_sems.at[1])
+        payload_copy.start()
+        payload_copy.wait()
     density_copy.wait()
 
 
@@ -459,19 +522,21 @@
     return pl.pallas_call(
         body,
         in_specs=[pl.BlockSpec(memory_space=pl.ANY) for _ in arrays],
-        out_specs=(pl.BlockSpec(memory_space=pl.ANY), pl.BlockSpec(memory_space=pl.ANY)),
+        out_specs=(
+            pl.BlockSpec(memory_space=pl.ANY),
+            pl.BlockSpec(memory_space=pltpu.VMEM if slot else pl.ANY),
+        ),
         out_shape=(
             jax.ShapeDtypeStruct(density, jnp.float32),
-            jax.ShapeDtypeStruct(payload, jnp.float32),
+            pltpu.VMEM(payload, jnp.float32) if slot else jax.ShapeDtypeStruct(payload, jnp.float32),
         ),
         scratch_shapes=[
             pltpu.SMEM((2 * ENTRIES,), jnp.int32),
-            pltpu.VMEM((KT * TILE, 2 * KT * TILE), jnp.bfloat16),
-            pltpu.VMEM(((KT - 1) * TILE, 2 * KT * TILE), jnp.bfloat16),
+            pltpu.VMEM(((2 * KT - 1) * TILE, 2 * KT * TILE), jnp.bfloat16),
             pltpu.VMEM((4, DEVICES, 8, TILE), jnp.int32),
             pltpu.VMEM((PTS, KT * TILE), jnp.bfloat16),
             pltpu.VMEM(density, jnp.float32),
-            pltpu.VMEM(payload, jnp.float32),
+            pltpu.VMEM((8, TILE) if slot else payload, jnp.float32),
             pltpu.VMEM((8, TILE), jnp.float32),
             pltpu.VMEM((3, 2, PTS), jnp.float32),
             pltpu.VMEM((2, PTS), jnp.float32),
@@ -521,6 +586,7 @@
         out_shape=jax.ShapeDtypeStruct((9, 2, ATOMS), jnp.float32),
         in_specs=[pl.BlockSpec(memory_space=pltpu.VMEM)],
         out_specs=pl.BlockSpec(memory_space=pltpu.VMEM),
+        compiler_params=pltpu.CompilerParams(vmem_limit_bytes=8 * 1024 * 1024),
         name="moment_table",
     )(arrived)
 
@@ -542,11 +608,9 @@
 ):
     rows = spread(tile_list, tile_count, point_count, density_first, density_second)
     rows = exchange(rows.reshape(DEVICES, LINES, TILE)).reshape(DEVICES * LINES, TILE)
-    first, rest, unit = windows(rows)
-    with jax.named_scope("send_first"):
-        first = exchange(first)
-    with jax.named_scope("send_rest"):
-        rest = exchange(rest)
+    first, coded, starts, unit = windows(rows)
+    first = exchange(first)
+    rest = exchange(rest_windows(starts, coded))
 
     table = batch_tables(tile_list, tile_count, point_count)
     flat = basis.reshape(-1, KT * TILE)

time: 144 us -> 141 us (0.979)
  waiting for transfers between devices: 34.9 us -> 27.9 us
  blocking collectives: 50.7 us -> 52.7 us
  Pallas kernels: 44.3 us -> 46.2 us
    all_to_all x2, waiting for transfers between devices: 34.9 us -> 27.9 us  [exchange(): return lax.all_to_all(value, ROW_COL, 0, 0, tiled=True)]
    pallas_call x2, Pallas kernels: 30.8 us -> 35 us  [batch_call(): pl.pallas_call(body, in_specs=[pl.BlockSpec(memory_space=pl.ANY) for _ in...]
    all_to_all x2, blocking collectives: 50.7 us -> 52.7 us  [exchange(): return lax.all_to_all(value, ROW_COL, 0, 0, tiled=True)]
    pallas_call x2 -> x3, Pallas kernels: 9.83 us -> 8.41 us  [the longest x1 3.08 us: spread(): pl.pallas_call(spread_body, out_shape=pltpu.VMEM((DEVICES * LINES, TILE),...]
  transfers between devices with their start and end apart: 2 -> 2, of which waited for: 2 -> 2; matrix products, arithmetic and copies ran while one was open for 0% -> 0% of each run, Pallas kernels for 14% -> 19%
where the time goes in v3:
time: 141 us; the launch traced here: 138 us
  blocking collectives  52.7 us (37%)
  Pallas kernels  46.2 us (33%)
  waiting for transfers between devices  27.9 us (20%)
  starting transfers between devices  10.6 us (8%)
    all_to_all x2, blocking collectives, exchange(): return lax.all_to_all(value, ROW_COL, 0, 0, tiled=True)  52.7 us
    pallas_call x2, Pallas kernels, batch_call(): pl.pallas_call(body, in_specs=[pl.BlockSpec(memory_space=pl.ANY) for _ in...  35 us
    all_to_all x2, waiting for transfers between devices, exchange(): return lax.all_to_all(value, ROW_COL, 0, 0, tiled=True)  27.9 us
    all_to_all x2, starting transfers between devices, exchange(): return lax.all_to_all(value, ROW_COL, 0, 0, tiled=True)  10.6 us
    pallas_call x1, Pallas kernels, spread(): pl.pallas_call(spread_body, out_shape=pltpu.VMEM((DEVICES * LINES, TILE),...  3.08 us
  transfers between devices with their start and end apart: 2, of which 2 were waited for; matrix products, arithmetic and copies ran while one was open for 0% of the time, Pallas kernels for 19%

profile of v3, /device:TPU:1, one launch (start us, length us, event | category | flops | bytes accessed | tf_op | source)
XLA Modules:
  0.0 138.0 jit_solution(15675227337504634844)
XLA Ops:
  0.6 3.1 %spread_rows.1 = bf16[4096,128]{1,0:T(8,128)(2,1)S(1)} custom-call(s32[2,7]{1,0:T(2,128)} %list_in.1, s32[2]{0:T(128)} %tiles_in.1, s32[2]{0:T(128)} %points_in.1, bf16[768,1536]{1,0:T(8,128)(2,1)} %first.1, bf16[768,1536]{1,0:T(8,128)(2,1)} %second.1), custom_call_target="tpu_custom_call" | custom-call | tf_op jit(solution)/shard_map/spread_rows/pallas_call | solution.py:106
  3.7 30.1 %all_to_all.20 = bf16[128,32,128]{2,1,0:T(8,128)(2,1)S(1)} all-to-all(bf16[128,32,128]{2,1,0:T(8,128)(2,1)S(1)} %bitcast.6), channel_id=1, replica_groups=mesh['row_0'=4,'row_1'=4,'col_0'=4,'col_1'=2] {'row_0','row_1','col_0','..., dimensions={0} | all-to-all | bytes 2097152 | tf_op jit(solution)/shard_map/all_to_all | solution.py:595
  33.8 2.8 %pick_windows.1 = (s32[128,32,128]{2,1,0:T(8,128)}, s32[768,128]{1,0:T(8,128)}, s32[8,128]{1,0:T(8,128)}, f32[8,128]{1,0:T(8,128)}) custom-call(bf16[4096,128]{1,0:T(8,128)(2,1)S(1)} %bitcast.5), custom_call_target="tpu_custom_call" | custom-call | tf_op jit(solution)/shard_map/pick_windows/pallas_call | solution.py:228
  36.6 4.8 %all-to-all-start.1 = ((s32[128,32,128]{2,1,0:T(8,128)}), s32[128,32,128]{2,1,0:T(8,128)S(1)}, u32[]{:S(2)}, u32[]{:S(2)}) async-start(s32[128,32,128]{2,1,0:T(8,128)} %get-tuple-element.10), calls=%async_computation.1 | async-start | bytes 4194304 | tf_op jit(solution)/shard_map/all_to_all | solution.py:595
  41.4 1.8 %batch_tables.1.refs_0_ = s32[80]{0:T(128)} custom-call(s32[2,7]{1,0:T(2,128)} %list_in.1, s32[2]{0:T(128)} %tiles_in.1, s32[2]{0:T(128)} %points_in.1), custom_call_target="tpu_custom_call" | custom-call | tf_op jit(solution)/shard_map/batch_tables/pallas_call | solution.py:332
  43.2 2.6 %pick_rest.1 = s32[128,24,128]{2,1,0:T(8,128)} custom-call(s32[8,128]{1,0:T(8,128)} %get-tuple-element.11.starts, s32[768,128]{1,0:T(8,128)} %get-tuple-element.12.coded), custom_call_target="tpu_custom_call" | custom-call | tf_op jit(solution)/shard_map/pick_rest/pallas_call | solution.py:259
  45.7 25.9 %all-to-all-done.1.refs_1_ = s32[128,32,128]{2,1,0:T(8,128)S(1)} async-done(((s32[128,32,128]{2,1,0:T(8,128)}), s32[128,32,128]{2,1,0:T(8,128)S(1)}, u32[]{:S(2)}, u32[]{:S(2)}) %all-to-all-start.1) | async-done | bytes 2097184 | tf_op jit(solution)/shard_map/all_to_all | solution.py:595
  71.6 0.0 copy-start
  71.6 5.8 %all-to-all-start.2 = ((s32[128,24,128]{2,1,0:T(8,128)}), s32[128,24,128]{2,1,0:T(8,128)}, u32[]{:S(2)}, u32[]{:S(2)}) async-start(s32[128,24,128]{2,1,0:T(8,128)} %pick_rest.1), calls=%async_computation.2 | async-start | bytes 3145728 | tf_op jit(solution)/shard_map/all_to_all | solution.py:595
  77.4 0.0 copy-done
  77.4 22.2 %batch_density_0.1 = (f32[2,4096]{1,0:T(2,128)}, f32[2,128]{1,0:T(2,128)}) custom-call(s32[80]{0:T(128)} %batch_tables.1.refs_0_, s32[128,32,128]{2,1,0:T(8,128)} %copy-done, f32[8,128]{1,0:T(8,128)} %get-tuple-element.13.refs_2_.refs_5_, f32[3,2,4096]{2,1,0:T(2,128)} %refs_6_.1, f32[2,4096]{1,0:T(2,128)} %refs_7_.1, s32[2,4096]{1,0:T(2,128)} %refs_8_.1, ...), custom_call_target="tpu_custom_call" | custom-call | flops 25999998976 | bytes 10000000 | tf_op jit(solution)/shard_map/batch_density_0/pallas_call | solution.py:522
  99.6 2.0 %all-to-all-done.2.refs_2_ = s32[128,24,128]{2,1,0:T(8,128)} async-done(((s32[128,24,128]{2,1,0:T(8,128)}), s32[128,24,128]{2,1,0:T(8,128)}, u32[]{:S(2)}, u32[]{:S(2)}) %all-to-all-start.2) | async-done | bytes 1572896 | tf_op jit(solution)/shard_map/all_to_all | solution.py:595
  101.6 12.8 %batch_density_1.1 = (f32[2,2,4096]{2,1,0:T(2,128)}, f32[128,2,128]{2,1,0:T(2,128)S(1)}) custom-call(s32[80]{0:T(128)} %batch_tables.1.refs_0_, s32[128,32,128]{2,1,0:T(8,128)} %copy-done, s32[128,24,128]{2,1,0:T(8,128)} %all-to-all-done.2.refs_2_, f32[2,128]{1,0:T(2,128)} %get-tuple-element.14.refs_3_, f32[2,4096]{1,0:T(2,128)} %get-tuple-element.15.refs_4_, ...), custom_call_target="tpu_custom_call" | custom-call | flops 25999998976 | bytes 10000000 | tf_op jit(solution)/shard_map/batch_density_1/pallas_call | solution.py:522
  114.4 22.6 %all_to_all.21 = f32[128,2,128]{2,1,0:T(2,128)S(1)} all-to-all(f32[128,2,128]{2,1,0:T(2,128)S(1)} %get-tuple-element.17), channel_id=1, replica_groups=mesh['row_0'=4,'row_1'=4,'col_0'=4,'col_1'=2] {'row_0','row_1','col_0','..., dimensions={0} | all-to-all | bytes 262144 | tf_op jit(solution)/shard_map/all_to_all | solution.py:595
  137.0 1.0 moment_table.1
Async XLA Ops:
  36.6 35.1 %all-to-all-start.1 = ((s32[128,32,128]{2,1,0:T(8,128)}), s32[128,32,128]{2,1,0:T(8,128)S(1)}, u32[]{:S(2)}, u32[]{:S(2)}) async-start(s32[128,32,128]{2,1,0:T(8,128)} %get-tuple-element.10), calls=%async_computation.1 | async-start | bytes 4194304 | tf_op jit(solution)/shard_map/all_to_all | solution.py:595
  71.6 5.8 %copy-start = (s32[128,32,128]{2,1,0:T(8,128)}, s32[128,32,128]{2,1,0:T(8,128)S(1)}, u32[]{:S(2)}) copy-start(s32[128,32,128]{2,1,0:T(8,128)S(1)} %all-to-all-done.1.refs_1_) | copy-start | bytes 6291460
  71.6 30.0 %all-to-all-start.2 = ((s32[128,24,128]{2,1,0:T(8,128)}), s32[128,24,128]{2,1,0:T(8,128)}, u32[]{:S(2)}, u32[]{:S(2)}) async-start(s32[128,24,128]{2,1,0:T(8,128)} %pick_rest.1), calls=%async_computation.2 | async-start | bytes 3145728 | tf_op jit(solution)/shard_map/all_to_all | solution.py:595

commit v4 on v3

--- a/solution.py
+++ b/solution.py
@@ -23,10 +23,7 @@
 LINES = 32
 PAIRS = KT * (KT + 1) // 2
 WINDOW = 2 * PAIRS
-FIRST = 32
-REST = WINDOW - FIRST
 GROUPS = 4
-SLOT_LINES = 24
 FRONT = 1152
 BACK = 1536
 BLOCK = 512
@@ -194,27 +191,23 @@
     coded_copy = pltpu.make_async_copy(coded, coded_to, out_sems.at[1])
     coded_copy.start()
     copy.wait()
-    copies = fill_windows(starts, coded, out_first, first_out, 0, FIRST, out_sems)
+    copies = fill_windows(0, starts, coded, out_first, first_out, out_sems)
     for copy in [unit_copy, starts_copy, coded_copy, *copies]:
         copy.wait()
 
 
-def fill_windows(starts, coded, filled, out, begin, end, sems):
-    def fill(dest, carry):
-        for slot in range(2):
-            start = starts[slot, dest]
+def fill_windows(slot, starts, coded, filled, out, sems):
+    def fill(pair, carry):
+        for half in range(2):
+            start = starts[slot, 2 * pair + half]
             for last in range(KT):
-                low = slot * PAIRS + pair_start(last)
-                high = low + last + 1
-                top = max(low, begin)
-                bottom = min(high, end)
-                if top < bottom:
-                    words = coded[pl.ds(pl.multiple_of((start + last) * 8, 8), 8), :]
-                    filled[dest, top - begin : bottom - begin, :] = words[top - low : bottom - low]
+                words = coded[pl.ds(pl.multiple_of((start + last) * 8, 8), 8), :]
+                low = half * PAIRS + pair_start(last)
+                filled[pair, low : low + last + 1, :] = words[: last + 1]
         return carry
 
     copies = []
-    group = DEVICES // GROUPS
+    group = DEVICES // 2 // GROUPS
     for part in range(GROUPS):
         lax.fori_loop(part * group, (part + 1) * group, fill, 0, unroll=2)
         span = pl.ds(part * group, group)
@@ -228,7 +221,7 @@
     return pl.pallas_call(
         window_body,
         out_shape=(
-            pltpu.HBM((DEVICES, FIRST, TILE), jnp.int32),
+            pltpu.HBM((DEVICES // 2, WINDOW, TILE), jnp.int32),
             pltpu.HBM((NT * 8, TILE), jnp.int32),
             pltpu.HBM((8, TILE), jnp.int32),
             pltpu.HBM((8, TILE), jnp.float32),
@@ -240,7 +233,7 @@
             pltpu.VMEM((NT * 8, TILE), jnp.int32),
             pltpu.VMEM((8, TILE), jnp.int32),
             pltpu.SMEM((8, TILE), jnp.int32),
-            pltpu.VMEM((DEVICES, FIRST, TILE), jnp.int32),
+            pltpu.VMEM((DEVICES // 2, WINDOW, TILE), jnp.int32),
             pltpu.VMEM((8, TILE), jnp.float32),
             pltpu.SemaphoreType.DMA,
             pltpu.SemaphoreType.DMA((3 + GROUPS,)),
@@ -251,21 +244,21 @@
 
 
 def rest_body(starts, coded, out, filled, sems):
-    for copy in fill_windows(starts, coded, filled, out, FIRST, WINDOW, sems):
+    for copy in fill_windows(1, starts, coded, filled, out, sems):
         copy.wait()
 
 
 def rest_windows(starts, coded):
     return pl.pallas_call(
         rest_body,
-        out_shape=jax.ShapeDtypeStruct((DEVICES, REST, TILE), jnp.int32),
+        out_shape=jax.ShapeDtypeStruct((DEVICES // 2, WINDOW, TILE), jnp.int32),
         in_specs=[
             pl.BlockSpec(memory_space=pltpu.SMEM),
             pl.BlockSpec(memory_space=pltpu.VMEM),
         ],
         out_specs=pl.BlockSpec(memory_space=pl.ANY),
         scratch_shapes=[
-            pltpu.VMEM((DEVICES, REST, TILE), jnp.int32),
+            pltpu.VMEM((DEVICES // 2, WINDOW, TILE), jnp.int32),
             pltpu.SemaphoreType.DMA((3 + GROUPS,)),
         ],
         name="pick_rest",
@@ -323,9 +316,8 @@
             high = order_of[last]
             for first in range(last + 1):
                 low = order_of[first]
-                line = slot * (PAIRS - SLOT_LINES) + high * (high + 1) // 2 + high - low
-                line = jnp.where(last < count, line, SLOT_LINES)
-                table[base + LINE + pair_start(last) + first] = (line // 8) * (DEVICES * 8) + line % 8
+                line = high * (high + 1) // 2 + high - low
+                table[base + LINE + pair_start(last) + first] = jnp.where(last < count, line, 0)
 
 
 def batch_tables(tile_list, tile_count, point_count):
@@ -340,41 +332,26 @@
 
 
 def batch_body(slot, *refs):
-    table_in, first_rows = refs[:2]
+    table, rows = refs[:2]
     refs = refs[2:]
     if slot:
-        rest_rows, before_in, earlier_in = refs[:3]
-        refs = refs[3:]
-        sources = [first_rows.at[:, pl.ds(FIRST - 8, 8), :]]
-        sources += [rest_rows.at[:, pl.ds(8 * group, 8), :] for group in range(REST // 8)]
-    else:
-        sources = [first_rows.at[:, pl.ds(8 * group, 8), :] for group in range(FIRST // 8)]
-    unit_in, offsets_in, weights_in, atoms_in, basis, density_out, payload_out = refs[:7]
-    (
-        table, parts, rows, values_in, density, payload,
-        unit, offsets, weights, atoms, before, earlier, sums_kept,
-        table_sem, row_sems, value_sems, side_sems, out_sems,
-    ) = refs[7:]
+        before, earlier = refs[:2]
+        refs = refs[2:]
+    unit, offsets, weights, atoms, basis, density_out, payload = refs[:7]
+    parts, values_in, density, sums_kept = refs[7:11]
+    value_sems, out_sems = refs[11:13]
     base = slot * ENTRIES
     if slot:
-        payload = payload_out
-
-    table_copy = pltpu.make_async_copy(table_in, table, table_sem)
-    table_copy.start()
-    row_copies = [
-        pltpu.make_async_copy(source, rows.at[group], row_sems.at[group])
-        for group, source in enumerate(sources)
-    ]
-    for copy in row_copies:
-        copy.start()
-    pairs = [(unit_in, unit), (offsets_in, offsets), (weights_in, weights), (atoms_in, atoms)]
-    if slot:
-        pairs += [(before_in, before), (earlier_in, earlier)]
-    side_copies = [
-        pltpu.make_async_copy(source, target, side_sems.at[place])
-        for place, (source, target) in enumerate(pairs)
-    ]
-    table_copy.wait()
+        rows_here, row_sems = refs[13:]
+        row_copies = []
+        for group in range(4):
+            span = pl.ds(group * (DEVICES * PAIRS // 4), DEVICES * PAIRS // 4)
+            row_copies.append(
+                pltpu.make_async_copy(rows.at[span], rows_here.at[span], row_sems.at[group])
+            )
+        for copy in row_copies:
+            copy.start()
+        rows = rows_here
     count = table[base + COUNT]
     live_points = table[base + POINTS]
     base_atom = table[base + ATOM]
@@ -389,18 +366,16 @@
 
     for step in range(STEPS):
         pl.when(step * BLOCK < live_points)(lambda step=step: value_copy(step).start())
-    for copy in side_copies:
-        copy.start()
-    if not slot:
+    if slot:
+        for copy in row_copies:
+            copy.wait()
+    else:
         density[...] = jnp.zeros((2, PTS), jnp.float32)
-    for copy in row_copies:
-        copy.wait()
-    lines = rows.reshape(len(sources) * DEVICES * 8, TILE)
 
     def unpack(last):
         for first in range(last + 1):
             start = table[base + LINE + pair_start(last) + first]
-            words = lines[pl.ds(start, TILE, stride=8), :]
+            words = rows[pl.ds(start, TILE, stride=PAIRS), :]
             down = slice(first * TILE, (first + 1) * TILE)
             for matrix in range(2):
                 value = words >> 16 if matrix == 0 else (words << 16) >> 16
@@ -416,8 +391,6 @@
         unpack(last)
     for last in range(KT - 2, KT):
         pl.when(count > last)(lambda last=last: unpack(last))
-    for copy in side_copies:
-        copy.wait()
     if slot:
         which = lax.broadcasted_iota(jnp.int32, (2, PTS), 0)
         for matrix in range(2):
@@ -504,53 +477,49 @@
             payload[:, matrix : matrix + 1, :] = jnp.broadcast_to(line[None], (DEVICES, 1, TILE))
         else:
             payload[matrix : matrix + 1, :] = line
-    if not slot:
-        payload_copy = pltpu.make_async_copy(payload, payload_out, out_sems.at[1])
-        payload_copy.start()
-        payload_copy.wait()
     density_copy.wait()
 
 
 def batch_call(slot, table, rows, carried, unit, offsets, weights, atoms, basis):
-    arrays = [table, *rows, *carried, unit, offsets, weights, atoms, basis]
+    arrays = [table, rows, *carried, unit, offsets, weights, atoms, basis]
     payload = (DEVICES, 2, TILE) if slot else (2, TILE)
     density = (2, 2, PTS) if slot else (2, PTS)
+    own_rows = []
+    if slot:
+        own_rows = [
+            pltpu.VMEM((DEVICES * PAIRS, TILE), jnp.int32),
+            pltpu.SemaphoreType.DMA((4,)),
+        ]
 
     def body(*refs):
         batch_body(slot, *refs)
 
     return pl.pallas_call(
         body,
-        in_specs=[pl.BlockSpec(memory_space=pl.ANY) for _ in arrays],
+        in_specs=[
+            pl.BlockSpec(memory_space=pltpu.SMEM),
+            pl.BlockSpec(memory_space=pltpu.HBM if slot else pltpu.VMEM),
+            *[pl.BlockSpec(memory_space=pltpu.VMEM) for _ in arrays[2:-1]],
+            pl.BlockSpec(memory_space=pltpu.HBM),
+        ],
         out_specs=(
             pl.BlockSpec(memory_space=pl.ANY),
-            pl.BlockSpec(memory_space=pltpu.VMEM if slot else pl.ANY),
+            pl.BlockSpec(memory_space=pltpu.VMEM),
         ),
         out_shape=(
             jax.ShapeDtypeStruct(density, jnp.float32),
-            pltpu.VMEM(payload, jnp.float32) if slot else jax.ShapeDtypeStruct(payload, jnp.float32),
+            pltpu.VMEM(payload, jnp.float32),
         ),
         scratch_shapes=[
-            pltpu.SMEM((2 * ENTRIES,), jnp.int32),
             pltpu.VMEM(((2 * KT - 1) * TILE, 2 * KT * TILE), jnp.bfloat16),
-            pltpu.VMEM((4, DEVICES, 8, TILE), jnp.int32),
             pltpu.VMEM((PTS, KT * TILE), jnp.bfloat16),
             pltpu.VMEM(density, jnp.float32),
-            pltpu.VMEM((8, TILE) if slot else payload, jnp.float32),
-            pltpu.VMEM((8, TILE), jnp.float32),
-            pltpu.VMEM((3, 2, PTS), jnp.float32),
-            pltpu.VMEM((2, PTS), jnp.float32),
-            pltpu.VMEM((2, PTS), jnp.int32),
-            pltpu.VMEM((2, TILE), jnp.float32),
-            pltpu.VMEM((2, PTS), jnp.float32),
             pltpu.VMEM((2, BLOCK, TILE), jnp.float32),
-            pltpu.SemaphoreType.DMA,
-            pltpu.SemaphoreType.DMA((4,)),
             pltpu.SemaphoreType.DMA((STEPS,)),
-            pltpu.SemaphoreType.DMA((6,)),
-            pltpu.SemaphoreType.DMA((2,)),
+            pltpu.SemaphoreType.DMA((1,)),
+            *own_rows,
         ],
-        compiler_params=pltpu.CompilerParams(vmem_limit_bytes=60 * 1024 * 1024),
+        compiler_params=pltpu.CompilerParams(vmem_limit_bytes=48 * 1024 * 1024),
         cost_estimate=pl.CostEstimate(
             flops=26_000_000_000, bytes_accessed=10_000_000, transcendentals=0
         ),
@@ -595,6 +564,10 @@
     return lax.all_to_all(value, ROW_COL, 0, 0, tiled=True)
 
 
+def exchange_windows(rows):
+    return exchange(rows.reshape(DEVICES, PAIRS // 4, 4, TILE)).reshape(DEVICES * PAIRS, TILE)
+
+
 def local(
     density_first,
     density_second,
@@ -609,15 +582,15 @@
     rows = spread(tile_list, tile_count, point_count, density_first, density_second)
     rows = exchange(rows.reshape(DEVICES, LINES, TILE)).reshape(DEVICES * LINES, TILE)
     first, coded, starts, unit = windows(rows)
-    first = exchange(first)
-    rest = exchange(rest_windows(starts, coded))
+    first = exchange_windows(first)
+    rest = exchange_windows(rest_windows(starts, coded))
 
     table = batch_tables(tile_list, tile_count, point_count)
     flat = basis.reshape(-1, KT * TILE)
     side = (unit, offsets, weights, atom_of_point)
-    density_0, payload_0 = batch_call(0, table, (first,), (), *side, flat)
+    density_0, payload_0 = batch_call(0, table, first, (), *side, flat)
     density, payload = batch_call(
-        1, table, (first, rest), (payload_0, density_0), *side, flat
+        1, table, rest, (payload_0, density_0), *side, flat
     )
     moments = moment_table(exchange(payload).reshape(DEVICES * 2, TILE)).swapaxes(0, 1)
     return density, moments

time: 141 us -> 137 us (0.972); the launches traced: 138 us -> 138 us
  Pallas kernels: 46.2 us -> 33.3 us
  waiting for transfers between devices: 27.9 us -> 39.3 us
    pallas_call x4, Pallas kernels: 40.3 us -> 27.8 us  [the longest x2 22.8 us: batch_call(): pl.pallas_call(body, in_specs=[pl.BlockSpec(memory_space=pltpu.SMEM), pl....]
    all_to_all x2, waiting for transfers between devices: 27.9 us -> 39.3 us  [exchange(): return lax.all_to_all(value, ROW_COL, 0, 0, tiled=True)]
  transfers between devices with their start and end apart: 2 -> 2, of which waited for: 2 -> 2; matrix products, arithmetic and copies ran while one was open for 0% -> 0% of each run, Pallas kernels for 19% -> 11%
where the time goes in v4:
time: 137 us; the launch traced here: 138 us
  blocking collectives  53.5 us (39%)
  waiting for transfers between devices  39.3 us (29%)
  Pallas kernels  33.3 us (24%)
  starting transfers between devices  10.8 us (8%)
    all_to_all x2, blocking collectives, exchange(): return lax.all_to_all(value, ROW_COL, 0, 0, tiled=True)  53.5 us
    all_to_all x2, waiting for transfers between devices, exchange(): return lax.all_to_all(value, ROW_COL, 0, 0, tiled=True)  39.3 us
    pallas_call x2, Pallas kernels, batch_call(): pl.pallas_call(body, in_specs=[pl.BlockSpec(memory_space=pltpu.SMEM), pl....  22.8 us
    all_to_all x2, starting transfers between devices, exchange(): return lax.all_to_all(value, ROW_COL, 0, 0, tiled=True)  10.8 us
    pallas_call x1, Pallas kernels, spread(): pl.pallas_call(spread_body, out_shape=pltpu.VMEM((DEVICES * LINES, TILE),...  3.08 us
  transfers between devices with their start and end apart: 2, of which 2 were waited for; matrix products, arithmetic and copies ran while one was open for 0% of the time, Pallas kernels for 11%

profile of v4, /device:TPU:1, one launch (start us, length us, event | category | flops | bytes accessed | tf_op | source)
XLA Modules:
  0.0 137.6 jit_solution(16013143563395693130)
XLA Ops:
  0.6 3.1 %spread_rows.1 = bf16[4096,128]{1,0:T(8,128)(2,1)S(1)} custom-call(s32[2,7]{1,0:T(2,128)} %list_in.1, s32[2]{0:T(128)} %tiles_in.1, s32[2]{0:T(128)} %points_in.1, bf16[768,1536]{1,0:T(8,128)(2,1)} %first.1, bf16[768,1536]{1,0:T(8,128)(2,1)} %second.1), custom_call_target="tpu_custom_call" | custom-call | tf_op jit(solution)/shard_map/spread_rows/pallas_call | solution.py:103
  3.7 30.1 %all_to_all.20 = bf16[128,32,128]{2,1,0:T(8,128)(2,1)S(1)} all-to-all(bf16[128,32,128]{2,1,0:T(8,128)(2,1)S(1)} %bitcast.10), channel_id=1, replica_groups=mesh['row_0'=4,'row_1'=4,'col_0'=4,'col_1'=2] {'row_0','row_1','col_0','..., dimensions={0} | all-to-all | bytes 2097152 | tf_op jit(solution)/shard_map/all_to_all | solution.py:564
  33.8 2.5 %pick_windows.1 = (s32[64,56,128]{2,1,0:T(8,128)}, s32[768,128]{1,0:T(8,128)}, s32[8,128]{1,0:T(8,128)}, f32[8,128]{1,0:T(8,128)}) custom-call(bf16[4096,128]{1,0:T(8,128)(2,1)S(1)} %bitcast.9), custom_call_target="tpu_custom_call" | custom-call | tf_op jit(solution)/shard_map/pick_windows/pallas_call | solution.py:221
  36.3 4.8 %all-to-all-start.2 = ((s32[128,7,4,128]{3,2,1,0:T(4,128)}), s32[128,7,4,128]{3,2,1,0:T(4,128)S(1)}, u32[]{:S(2)}, u32[]{:S(2)}) async-start(s32[128,7,4,128]{3,2,1,0:T(4,128)} %bitcast.14), calls=%async_computation.2 | async-start | bytes 3670016 | tf_op jit(solution)/shard_map/all_to_all | solution.py:564
  41.1 1.5 %batch_tables.1.refs_0_ = s32[80]{0:T(128)} custom-call(s32[2,7]{1,0:T(2,128)} %list_in.1, s32[2]{0:T(128)} %tiles_in.1, s32[2]{0:T(128)} %points_in.1), custom_call_target="tpu_custom_call" | custom-call | tf_op jit(solution)/shard_map/batch_tables/pallas_call | solution.py:324
  42.6 2.5 %pick_rest.1 = s32[64,56,128]{2,1,0:T(8,128)} custom-call(s32[8,128]{1,0:T(8,128)} %get-tuple-element.10.starts, s32[768,128]{1,0:T(8,128)} %get-tuple-element.11.coded), custom_call_target="tpu_custom_call" | custom-call | tf_op jit(solution)/shard_map/pick_rest/pallas_call | solution.py:252
  45.1 23.4 %all-to-all-done.2 = s32[128,7,4,128]{3,2,1,0:T(4,128)S(1)} async-done(((s32[128,7,4,128]{3,2,1,0:T(4,128)}), s32[128,7,4,128]{3,2,1,0:T(4,128)S(1)}, u32[]{:S(2)}, u32[]{:S(2)}) %all-to-all-start.2) | async-done | bytes 1835040 | tf_op jit(solution)/shard_map/all_to_all | solution.py:564
  68.5 0.0 copy-start
  68.5 0.0 copy-start.1
  68.5 0.0 copy-start.2
  68.5 0.0 copy-start.3
  68.5 0.0 copy-start.4
  68.5 6.0 %all-to-all-start.1 = ((s32[128,7,4,128]{3,2,1,0:T(4,128)}), s32[128,7,4,128]{3,2,1,0:T(4,128)}, u32[]{:S(2)}, u32[]{:S(2)}) async-start(s32[128,7,4,128]{3,2,1,0:T(4,128)} %bitcast.13), calls=%async_computation.1 | async-start | bytes 3670016 | tf_op jit(solution)/shard_map/all_to_all | solution.py:564
  74.5 0.0 copy-done
  74.5 0.0 copy-done.1
  74.5 0.0 copy-done.2
  74.5 0.0 copy-done.3
  74.5 0.0 copy-done.4
  74.5 11.2 %batch_density_0.1 = (f32[2,4096]{1,0:T(2,128)S(1)}, f32[2,128]{1,0:T(2,128)S(1)}) custom-call(s32[80]{0:T(128)S(1)} %copy-done, s32[3584,128]{1,0:T(8,128)S(1)} %bitcast.11, f32[8,128]{1,0:T(8,128)S(1)} %copy-done.4, f32[3,2,4096]{2,1,0:T(2,128)S(1)} %copy-done.1, f32[2,4096]{1,0:T(2,128)S(1)} %copy-done.2, s32[2,4096]{1,0:T(2,128)S(1)} %copy-done.3, ...), custom_call_target="tpu_custom_call" | custom-call | flops 25999998976 | bytes 10000000 | tf_op jit(solution)/shard_map/batch_density_0/pallas_call | solution.py:497
  85.7 15.8 %all-to-all-done.1 = s32[128,7,4,128]{3,2,1,0:T(4,128)} async-done(((s32[128,7,4,128]{3,2,1,0:T(4,128)}), s32[128,7,4,128]{3,2,1,0:T(4,128)}, u32[]{:S(2)}, u32[]{:S(2)}) %all-to-all-start.1) | async-done | bytes 1835040 | tf_op jit(solution)/shard_map/all_to_all | solution.py:564
  101.6 11.6 %batch_density_1.1 = (f32[2,2,4096]{2,1,0:T(2,128)}, f32[128,2,128]{2,1,0:T(2,128)S(1)}) custom-call(s32[80]{0:T(128)S(1)} %copy-done, s32[3584,128]{1,0:T(8,128)} %bitcast.3.refs_1_, f32[2,128]{1,0:T(2,128)S(1)} %get-tuple-element.14.refs_2_, f32[2,4096]{1,0:T(2,128)S(1)} %get-tuple-element.15.refs_3_, f32[8,128]{1,0:T(8,128)S(1)} %copy-done.4, ...), custom_call_target="tpu_custom_call" | custom-call | flops 25999998976 | bytes 10000000 | tf_op jit(solution)/shard_map/batch_density_1/pallas_call | solution.py:497
  113.2 23.5 %all_to_all.21 = f32[128,2,128]{2,1,0:T(2,128)S(1)} all-to-all(f32[128,2,128]{2,1,0:T(2,128)S(1)} %get-tuple-element.17), channel_id=1, replica_groups=mesh['row_0'=4,'row_1'=4,'col_0'=4,'col_1'=2] {'row_0','row_1','col_0','..., dimensions={0} | all-to-all | bytes 262144 | tf_op jit(solution)/shard_map/all_to_all | solution.py:564
  136.6 1.0 moment_table.1
Async XLA Ops:
  36.3 32.2 %all-to-all-start.2 = ((s32[128,7,4,128]{3,2,1,0:T(4,128)}), s32[128,7,4,128]{3,2,1,0:T(4,128)S(1)}, u32[]{:S(2)}, u32[]{:S(2)}) async-start(s32[128,7,4,128]{3,2,1,0:T(4,128)} %bitcast.14), calls=%async_computation.2 | async-start | bytes 3670016 | tf_op jit(solution)/shard_map/all_to_all | solution.py:564
  68.5 6.0 %copy-start = (s32[80]{0:T(128)S(1)}, s32[80]{0:T(128)}, u32[]{:S(2)}) copy-start(s32[80]{0:T(128)} %batch_tables.1.refs_0_) | copy-start | bytes 964
  68.5 6.0 %copy-start.1 = (f32[3,2,4096]{2,1,0:T(2,128)S(1)}, f32[3,2,4096]{2,1,0:T(2,128)}, u32[]{:S(2)}) copy-start(f32[3,2,4096]{2,1,0:T(2,128)} %refs_5_.3) | copy-start | bytes 294916
  68.5 6.0 %copy-start.2 = (f32[2,4096]{1,0:T(2,128)S(1)}, f32[2,4096]{1,0:T(2,128)}, u32[]{:S(2)}) copy-start(f32[2,4096]{1,0:T(2,128)} %refs_6_.1) | copy-start | bytes 98308
  68.5 6.0 %copy-start.3 = (s32[2,4096]{1,0:T(2,128)S(1)}, s32[2,4096]{1,0:T(2,128)}, u32[]{:S(2)}) copy-start(s32[2,4096]{1,0:T(2,128)} %refs_7_.1) | copy-start | bytes 98308
  68.5 6.0 %copy-start.4 = (f32[8,128]{1,0:T(8,128)S(1)}, f32[8,128]{1,0:T(8,128)}, u32[]{:S(2)}) copy-start(f32[8,128]{1,0:T(8,128)} %get-tuple-element.13.refs_2_.refs_4_) | copy-start | bytes 12292
  68.5 33.0 %all-to-all-start.1 = ((s32[128,7,4,128]{3,2,1,0:T(4,128)}), s32[128,7,4,128]{3,2,1,0:T(4,128)}, u32[]{:S(2)}, u32[]{:S(2)}) async-start(s32[128,7,4,128]{3,2,1,0:T(4,128)} %bitcast.13), calls=%async_computation.1 | async-start | bytes 3670016 | tf_op jit(solution)/shard_map/all_to_all | solution.py:564

commit v5 on v4

--- a/solution.py
+++ b/solution.py
@@ -20,7 +20,7 @@
 ROW_COL = ("row_0", "row_1", "col_0", "col_1")
 
 SLOTS = 24
-LINES = 32
+LINES = 28
 PAIRS = KT * (KT + 1) // 2
 WINDOW = 2 * PAIRS
 GROUPS = 4
@@ -80,23 +80,23 @@
         copy.wait()
     own_start = [least_tile(tile_list, batch) for batch in slot_order(tile_count, point_count)]
     peak = jnp.max(largest)
-    line = lax.broadcasted_iota(jnp.int32, (8, TILE), 0)
+    line = lax.broadcasted_iota(jnp.int32, (4, TILE), 0)
     extra = jnp.where(
         line == 0,
         own_start[0].astype(jnp.float32),
         jnp.where(line == 1, own_start[1].astype(jnp.float32), peak),
     )
 
-    def pack(dest, carry):
-        at = pl.multiple_of(dest * SLOTS, 8)
-        low = lines[pl.ds(at, 16), :]
-        high = lines[pl.ds(at + 16, 8), :]
-        to = pl.multiple_of(dest * LINES, 16)
-        out[pl.ds(to, 16), :] = low.astype(jnp.bfloat16)
-        out[pl.ds(to + 16, 16), :] = jnp.concatenate([high, extra], axis=0).astype(jnp.bfloat16)
+    def pack(group, carry):
+        pieces = []
+        for dest in range(4):
+            at = pl.multiple_of((group * 4 + dest) * SLOTS, 8)
+            pieces += [lines[pl.ds(at, SLOTS), :], extra]
+        to = pl.multiple_of(group * 4 * LINES, 16)
+        out[pl.ds(to, 4 * LINES), :] = jnp.concatenate(pieces, axis=0).astype(jnp.bfloat16)
         return carry
 
-    lax.fori_loop(0, DEVICES, pack, 0, unroll=4)
+    lax.fori_loop(0, DEVICES // 4, pack, 0, unroll=2)
 
 
 def spread(tile_list, tile_count, point_count, first, second):
@@ -127,22 +127,24 @@
     arrived, first_out, coded_to, starts_to, unit_to,
     lines, coded, start_lines, starts, out_first, unit_out, sem, out_sems,
 ):
-    def widen(source, top):
-        at = pl.multiple_of(source * LINES, 16)
-        to = pl.multiple_of(FRONT + source * SLOTS, 8)
-        low = arrived[pl.ds(at, 16), :].astype(jnp.float32)
-        high = arrived[pl.ds(at + 16, 16), :].astype(jnp.float32)
-        lines[pl.ds(to, 16), :] = low
-        lines[pl.ds(to + 16, 8), :] = high[0:8]
-        extra = high[8:16]
+    def widen(group, top):
         peak, own = top
-        lane = lax.broadcasted_iota(jnp.int32, (8, TILE), 1)
-        own = jnp.where(lane == source, extra, own)
-        return jnp.maximum(peak, extra), own
-
-    zero = jnp.zeros((8, TILE), jnp.float32)
-    tops, own = lax.fori_loop(0, DEVICES, widen, (zero, zero), unroll=4)
-    start_lines[...] = own.astype(jnp.int32)
+        lane = lax.broadcasted_iota(jnp.int32, (4, TILE), 1)
+        at = pl.multiple_of(group * 4 * LINES, 16)
+        block = arrived[pl.ds(at, 4 * LINES), :].astype(jnp.float32)
+        for place in range(4):
+            source = group * 4 + place
+            to = pl.multiple_of(FRONT + source * SLOTS, 8)
+            lines[pl.ds(to, SLOTS), :] = block[place * LINES : place * LINES + SLOTS]
+            extra = block[place * LINES + SLOTS : (place + 1) * LINES]
+            own = jnp.where(lane == source, extra, own)
+            peak = jnp.maximum(peak, extra)
+        return peak, own
+
+    zero = jnp.zeros((4, TILE), jnp.float32)
+    tops, own = lax.fori_loop(0, DEVICES // 4, widen, (zero, zero), unroll=2)
+    start_lines[0:4, :] = own.astype(jnp.int32)
+    start_lines[4:8, :] = jnp.zeros((4, TILE), jnp.int32)
     copy = pltpu.make_async_copy(start_lines, starts, sem)
     copy.start()
     starts_copy = pltpu.make_async_copy(start_lines, starts_to, out_sems.at[2])
@@ -366,17 +368,15 @@
 
     for step in range(STEPS):
         pl.when(step * BLOCK < live_points)(lambda step=step: value_copy(step).start())
-    if slot:
-        for copy in row_copies:
-            copy.wait()
-    else:
+    if not slot:
         density[...] = jnp.zeros((2, PTS), jnp.float32)
 
-    def unpack(last):
+    def unpack(last, part, size):
         for first in range(last + 1):
-            start = table[base + LINE + pair_start(last) + first]
-            words = rows[pl.ds(start, TILE, stride=PAIRS), :]
-            down = slice(first * TILE, (first + 1) * TILE)
+            start = table[base + LINE + pair_start(last) + first] + part * size * PAIRS
+            words = rows[pl.ds(start, size, stride=PAIRS), :]
+            down = slice(first * TILE + part * size, first * TILE + (part + 1) * size)
+            low = (last + 1 + first) * TILE + part * size
             for matrix in range(2):
                 value = words >> 16 if matrix == 0 else (words << 16) >> 16
                 value = value.astype(jnp.float32)
@@ -385,12 +385,17 @@
                 parts[down, at : at + TILE] = top
                 if first < last:
                     bottom = (value - top.astype(jnp.float32)).astype(jnp.bfloat16)
-                    parts[(last + 1 + first) * TILE : (last + 2 + first) * TILE, at : at + TILE] = bottom
-
-    for last in range(KT - 2):
-        unpack(last)
-    for last in range(KT - 2, KT):
-        pl.when(count > last)(lambda last=last: unpack(last))
+                    parts[low : low + size, at : at + TILE] = bottom
+
+    pieces = 4 if slot else 1
+    for part in range(pieces):
+        if slot:
+            row_copies[part].wait()
+        size = TILE // pieces
+        for last in range(KT - 2):
+            unpack(last, part, size)
+        for last in range(KT - 2, KT):
+            pl.when(count > last)(lambda last=last: unpack(last, part, size))
     if slot:
         which = lax.broadcasted_iota(jnp.int32, (2, PTS), 0)
         for matrix in range(2):
@@ -564,8 +569,8 @@
     return lax.all_to_all(value, ROW_COL, 0, 0, tiled=True)
 
 
-def exchange_windows(rows):
-    return exchange(rows.reshape(DEVICES, PAIRS // 4, 4, TILE)).reshape(DEVICES * PAIRS, TILE)
+def exchange_lines(rows):
+    return exchange(rows.reshape(DEVICES, -1, 4, TILE)).reshape(-1, TILE)
 
 
 def local(
@@ -580,10 +585,10 @@
     atom_of_point,
 ):
     rows = spread(tile_list, tile_count, point_count, density_first, density_second)
-    rows = exchange(rows.reshape(DEVICES, LINES, TILE)).reshape(DEVICES * LINES, TILE)
+    rows = exchange_lines(rows)
     first, coded, starts, unit = windows(rows)
-    first = exchange_windows(first)
-    rest = exchange_windows(rest_windows(starts, coded))
+    first = exchange_lines(first)
+    rest = exchange_lines(rest_windows(starts, coded))
 
     table = batch_tables(tile_list, tile_count, point_count)
     flat = basis.reshape(-1, KT * TILE)

time: 137 us -> 133 us (0.971)
  Pallas kernels: 33.3 us -> 44.6 us
  waiting for transfers between devices: 39.3 us -> 30.9 us
  blocking collectives: 53.5 us -> 46.4 us
    pallas_call x2, Pallas kernels: 22.8 us -> 34.5 us  [batch_call(): pl.pallas_call(body, in_specs=[pl.BlockSpec(memory_space=pltpu.SMEM), pl....]
    all_to_all x2, waiting for transfers between devices: 39.3 us -> 30.9 us  [exchange(): return lax.all_to_all(value, ROW_COL, 0, 0, tiled=True)]
    all_to_all x2, blocking collectives: 53.5 us -> 46.4 us  [exchange(): return lax.all_to_all(value, ROW_COL, 0, 0, tiled=True)]
  transfers between devices with their start and end apart: 2 -> 2, of which waited for: 2 -> 2; matrix products, arithmetic and copies ran while one was open for 0% -> 0% of each run, Pallas kernels for 11% -> 18%
where the time goes in v5:
time: 133 us
  blocking collectives  46.4 us (35%)
  Pallas kernels  44.6 us (34%)
  waiting for transfers between devices  30.9 us (23%)
  starting transfers between devices  10.7 us (8%)
    all_to_all x2, blocking collectives, exchange(): return lax.all_to_all(value, ROW_COL, 0, 0, tiled=True)  46.4 us
    pallas_call x2, Pallas kernels, batch_call(): pl.pallas_call(body, in_specs=[pl.BlockSpec(memory_space=pltpu.SMEM), pl....  34.5 us
    all_to_all x2, waiting for transfers between devices, exchange(): return lax.all_to_all(value, ROW_COL, 0, 0, tiled=True)  30.9 us
    all_to_all x2, starting transfers between devices, exchange(): return lax.all_to_all(value, ROW_COL, 0, 0, tiled=True)  10.7 us
    pallas_call x1, Pallas kernels, spread(): pl.pallas_call(spread_body, out_shape=pltpu.VMEM((DEVICES * LINES, TILE),...  2.82 us
  transfers between devices with their start and end apart: 2, of which 2 were waited for; matrix products, arithmetic and copies ran while one was open for 0% of the time, Pallas kernels for 18%

profile of v5, /device:TPU:1, one launch (start us, length us, event | category | flops | bytes accessed | tf_op | source)
XLA Modules:
  0.0 133.3 jit_solution(14303156396442791511)
XLA Ops:
  0.6 2.8 %spread_rows.1 = bf16[3584,128]{1,0:T(8,128)(2,1)S(1)} custom-call(s32[2,7]{1,0:T(2,128)} %list_in.1, s32[2]{0:T(128)} %tiles_in.1, s32[2]{0:T(128)} %points_in.1, bf16[768,1536]{1,0:T(8,128)(2,1)} %first.1, bf16[768,1536]{1,0:T(8,128)(2,1)} %second.1), custom_call_target="tpu_custom_call" | custom-call | tf_op jit(solution)/shard_map/spread_rows/pallas_call | solution.py:103
  3.5 28.8 %all_to_all.20 = bf16[128,7,4,128]{3,2,1,0:T(4,128)(2,1)S(1)} all-to-all(bf16[128,7,4,128]{3,2,1,0:T(4,128)(2,1)S(1)} %bitcast.9), channel_id=1, replica_groups=mesh['row_0'=4,'row_1'=4,'col_0'=4,'col_1'=2] {'row_0','row_1','col_0','..., dimensions={0} | all-to-all | bytes 1835008 | tf_op jit(solution)/shard_map/all_to_all | solution.py:569
  32.2 2.3 %pick_windows.1 = (s32[64,56,128]{2,1,0:T(8,128)}, s32[768,128]{1,0:T(8,128)}, s32[8,128]{1,0:T(8,128)}, f32[8,128]{1,0:T(8,128)}) custom-call(bf16[3584,128]{1,0:T(8,128)(2,1)S(1)} %bitcast.10), custom_call_target="tpu_custom_call" | custom-call | tf_op jit(solution)/shard_map/pick_windows/pallas_call | solution.py:223
  34.6 4.7 %all-to-all-start.2 = ((s32[128,7,4,128]{3,2,1,0:T(4,128)}), s32[128,7,4,128]{3,2,1,0:T(4,128)S(1)}, u32[]{:S(2)}, u32[]{:S(2)}) async-start(s32[128,7,4,128]{3,2,1,0:T(4,128)} %bitcast.14), calls=%async_computation.2 | async-start | bytes 3670016 | tf_op jit(solution)/shard_map/all_to_all | solution.py:569
  39.3 1.5 %batch_tables.1.refs_0_ = s32[80]{0:T(128)} custom-call(s32[2,7]{1,0:T(2,128)} %list_in.1, s32[2]{0:T(128)} %tiles_in.1, s32[2]{0:T(128)} %points_in.1), custom_call_target="tpu_custom_call" | custom-call | tf_op jit(solution)/shard_map/batch_tables/pallas_call | solution.py:326
  40.8 2.5 %pick_rest.1 = s32[64,56,128]{2,1,0:T(8,128)} custom-call(s32[8,128]{1,0:T(8,128)} %get-tuple-element.10.starts, s32[768,128]{1,0:T(8,128)} %get-tuple-element.11.coded), custom_call_target="tpu_custom_call" | custom-call | tf_op jit(solution)/shard_map/pick_rest/pallas_call | solution.py:254
  43.2 23.4 %all-to-all-done.2 = s32[128,7,4,128]{3,2,1,0:T(4,128)S(1)} async-done(((s32[128,7,4,128]{3,2,1,0:T(4,128)}), s32[128,7,4,128]{3,2,1,0:T(4,128)S(1)}, u32[]{:S(2)}, u32[]{:S(2)}) %all-to-all-start.2) | async-done | bytes 1835040 | tf_op jit(solution)/shard_map/all_to_all | solution.py:569
  66.7 0.0 copy-start
  66.7 0.0 copy-start.1
  66.7 0.0 copy-start.2
  66.7 0.0 copy-start.3
  66.7 0.0 copy-start.4
  66.7 6.0 %all-to-all-start.1 = ((s32[128,7,4,128]{3,2,1,0:T(4,128)}), s32[128,7,4,128]{3,2,1,0:T(4,128)}, u32[]{:S(2)}, u32[]{:S(2)}) async-start(s32[128,7,4,128]{3,2,1,0:T(4,128)} %bitcast.13), calls=%async_computation.1 | async-start | bytes 3670016 | tf_op jit(solution)/shard_map/all_to_all | solution.py:569
  72.6 0.0 copy-done
  72.6 0.0 copy-done.1
  72.7 0.0 copy-done.2
  72.7 0.0 copy-done.3
  72.7 0.0 copy-done.4
  72.7 19.5 %batch_density_0.1 = (f32[2,4096]{1,0:T(2,128)S(1)}, f32[2,128]{1,0:T(2,128)S(1)}) custom-call(s32[80]{0:T(128)S(1)} %copy-done, s32[3584,128]{1,0:T(8,128)S(1)} %bitcast.11, f32[8,128]{1,0:T(8,128)S(1)} %copy-done.4, f32[3,2,4096]{2,1,0:T(2,128)S(1)} %copy-done.1, f32[2,4096]{1,0:T(2,128)S(1)} %copy-done.2, s32[2,4096]{1,0:T(2,128)S(1)} %copy-done.3, ...), custom_call_target="tpu_custom_call" | custom-call | flops 25999998976 | bytes 10000000 | tf_op jit(solution)/shard_map/batch_density_0/pallas_call | solution.py:502
  92.2 7.5 %all-to-all-done.1 = s32[128,7,4,128]{3,2,1,0:T(4,128)} async-done(((s32[128,7,4,128]{3,2,1,0:T(4,128)}), s32[128,7,4,128]{3,2,1,0:T(4,128)}, u32[]{:S(2)}, u32[]{:S(2)}) %all-to-all-start.1) | async-done | bytes 1835040 | tf_op jit(solution)/shard_map/all_to_all | solution.py:569
  99.7 15.0 %batch_density_1.1 = (f32[2,2,4096]{2,1,0:T(2,128)}, f32[128,2,128]{2,1,0:T(2,128)S(1)}) custom-call(s32[80]{0:T(128)S(1)} %copy-done, s32[3584,128]{1,0:T(8,128)} %bitcast.3.refs_1_, f32[2,128]{1,0:T(2,128)S(1)} %get-tuple-element.14.refs_2_, f32[2,4096]{1,0:T(2,128)S(1)} %get-tuple-element.15.refs_3_, f32[8,128]{1,0:T(8,128)S(1)} %copy-done.4, ...), custom_call_target="tpu_custom_call" | custom-call | flops 25999998976 | bytes 10000000 | tf_op jit(solution)/shard_map/batch_density_1/pallas_call | solution.py:502
  114.7 17.6 %all_to_all.21 = f32[128,2,128]{2,1,0:T(2,128)S(1)} all-to-all(f32[128,2,128]{2,1,0:T(2,128)S(1)} %get-tuple-element.17), channel_id=1, replica_groups=mesh['row_0'=4,'row_1'=4,'col_0'=4,'col_1'=2] {'row_0','row_1','col_0','..., dimensions={0} | all-to-all | bytes 262144 | tf_op jit(solution)/shard_map/all_to_all | solution.py:569
  132.3 1.0 moment_table.1
Async XLA Ops:
  34.6 32.1 %all-to-all-start.2 = ((s32[128,7,4,128]{3,2,1,0:T(4,128)}), s32[128,7,4,128]{3,2,1,0:T(4,128)S(1)}, u32[]{:S(2)}, u32[]{:S(2)}) async-start(s32[128,7,4,128]{3,2,1,0:T(4,128)} %bitcast.14), calls=%async_computation.2 | async-start | bytes 3670016 | tf_op jit(solution)/shard_map/all_to_all | solution.py:569
  66.7 6.0 %copy-start = (s32[80]{0:T(128)S(1)}, s32[80]{0:T(128)}, u32[]{:S(2)}) copy-start(s32[80]{0:T(128)} %batch_tables.1.refs_0_) | copy-start | bytes 964
  66.7 6.0 %copy-start.1 = (f32[3,2,4096]{2,1,0:T(2,128)S(1)}, f32[3,2,4096]{2,1,0:T(2,128)}, u32[]{:S(2)}) copy-start(f32[3,2,4096]{2,1,0:T(2,128)} %refs_5_.3) | copy-start | bytes 294916
  66.7 6.0 %copy-start.2 = (f32[2,4096]{1,0:T(2,128)S(1)}, f32[2,4096]{1,0:T(2,128)}, u32[]{:S(2)}) copy-start(f32[2,4096]{1,0:T(2,128)} %refs_6_.1) | copy-start | bytes 98308
  66.7 6.0 %copy-start.3 = (s32[2,4096]{1,0:T(2,128)S(1)}, s32[2,4096]{1,0:T(2,128)}, u32[]{:S(2)}) copy-start(s32[2,4096]{1,0:T(2,128)} %refs_7_.1) | copy-start | bytes 98308
  66.7 6.0 %copy-start.4 = (f32[8,128]{1,0:T(8,128)S(1)}, f32[8,128]{1,0:T(8,128)}, u32[]{:S(2)}) copy-start(f32[8,128]{1,0:T(8,128)} %get-tuple-element.13.refs_2_.refs_4_) | copy-start | bytes 12292
  66.7 33.0 %all-to-all-start.1 = ((s32[128,7,4,128]{3,2,1,0:T(4,128)}), s32[128,7,4,128]{3,2,1,0:T(4,128)}, u32[]{:S(2)}, u32[]{:S(2)}) async-start(s32[128,7,4,128]{3,2,1,0:T(4,128)} %bitcast.13), calls=%async_computation.1 | async-start | bytes 3670016 | tf_op jit(solution)/shard_map/all_to_all | solution.py:569

commit v6 on v5

--- a/solution.py
+++ b/solution.py
@@ -340,11 +340,11 @@
         before, earlier = refs[:2]
         refs = refs[2:]
     unit, offsets, weights, atoms, basis, density_out, payload = refs[:7]
-    parts, values_in, density, sums_kept = refs[7:11]
-    value_sems, out_sems = refs[11:13]
+    parts, values_in, density, sums_kept, atom_sums = refs[7:12]
+    value_sems, out_sems = refs[12:14]
     base = slot * ENTRIES
     if slot:
-        rows_here, row_sems = refs[13:]
+        rows_here, row_sems = refs[14:]
         row_copies = []
         for group in range(4):
             span = pl.ds(group * (DEVICES * PAIRS // 4), DEVICES * PAIRS // 4)
@@ -387,6 +387,7 @@
                     bottom = (value - top.astype(jnp.float32)).astype(jnp.bfloat16)
                     parts[low : low + size, at : at + TILE] = bottom
 
+    atom_sums[...] = jnp.zeros((16, 16, TILE), jnp.float32)
     pieces = 4 if slot else 1
     for part in range(pieces):
         if slot:
@@ -404,11 +405,24 @@
 
     blocks = (live_points + BLOCK - 1) // BLOCK
 
-    def reduce(step):
+    def reduce(step, valid):
         start = pl.multiple_of(step * BLOCK, BLOCK)
         point = start + lax.broadcasted_iota(jnp.int32, (1, BLOCK), 1)
         scale = jnp.where(point < live_points, unit[0:1, 0:1], 0.0)
         at = pl.ds(start, BLOCK)
+        mine = pl.ds(batch, 1)
+        x = offsets[0, mine, at]
+        y = offsets[1, mine, at]
+        z = offsets[2, mine, at]
+        weight = weights[mine, at]
+        near = lax.rem(atoms[mine, at] - base_atom + 2 * ATOMS, ATOMS)
+        near = jnp.where(valid, near, -1)
+        squared = x * x + y * y + z * z
+        shapes = [
+            jnp.ones_like(x), x, y, z, x * y, y * z,
+            3.0 * z * z - squared, x * z, x * x - y * y,
+        ]
+        shapes = jnp.concatenate([weight * shape for shape in shapes], axis=0)
         for matrix in range(2):
             pieces = [
                 jnp.sum(sums_kept[matrix, cut : cut + TILE, :].T, axis=0, keepdims=True)
@@ -419,11 +433,18 @@
                 density[matrix, pl.ds(batch, 1), at] = line
             else:
                 density[matrix : matrix + 1, at] = line
+            terms = line * shapes
+            for atom in range(8):
+                picked = jnp.where(near == atom, terms, 0.0)
+                total = picked[:, :TILE]
+                for cut in range(TILE, BLOCK, TILE):
+                    total = total + picked[:, cut : cut + TILE]
+                atom_sums[matrix * 8 + atom, :9, :] += total
 
     def densities(tiles):
         def block(step, carry):
             value_copy(step).wait()
-            reduce(jnp.maximum(step - 1, 0))
+            reduce(jnp.maximum(step - 1, 0), step > 0)
             start = pl.multiple_of(step * BLOCK, BLOCK)
             columns = []
             for place in range(tiles):
@@ -450,31 +471,17 @@
 
     for tiles in range(KT - 2, KT + 1):
         pl.when(count == tiles)(lambda tiles=tiles: densities(tiles))
-    reduce(jnp.maximum(blocks - 1, 0))
+    reduce(jnp.maximum(blocks - 1, 0), blocks > 0)
 
     density_copy = pltpu.make_async_copy(density, density_out, out_sems.at[0])
     density_copy.start()
-    mine = pl.ds(batch, 1)
-    x = offsets[0, mine, :]
-    y = offsets[1, mine, :]
-    z = offsets[2, mine, :]
-    weight = weights[mine, :]
-    near = lax.rem(atoms[mine, :] - base_atom + 2 * ATOMS, ATOMS)
-    squared = x * x + y * y + z * z
-    shapes = [
-        jnp.ones_like(x), x, y, z, x * y, y * z,
-        3.0 * z * z - squared, x * z, x * x - y * y,
-    ]
-    shapes = jnp.concatenate([weight * shape for shape in shapes], axis=0)
     lane = lax.broadcasted_iota(jnp.int32, (9, TILE), 1)
     degree = lax.broadcasted_iota(jnp.int32, (9, TILE), 0)
     lane = lane - degree * SPAN - 4 * batch
     for matrix in range(2):
-        terms = density[matrix, mine, :] if slot else density[matrix : matrix + 1, :]
-        terms = terms * shapes
         total = jnp.zeros((9, TILE), jnp.float32)
         for atom in range(8):
-            picked = jnp.sum(jnp.where(near == atom, terms, 0.0), axis=1, keepdims=True)
+            picked = jnp.sum(atom_sums[matrix * 8 + atom, :9, :], axis=1, keepdims=True)
             total = total + jnp.where(lane == atom, picked, 0.0)
         line = jnp.sum(total, axis=0, keepdims=True)
         if slot:
@@ -520,6 +527,7 @@
             pltpu.VMEM((PTS, KT * TILE), jnp.bfloat16),
             pltpu.VMEM(density, jnp.float32),
             pltpu.VMEM((2, BLOCK, TILE), jnp.float32),
+            pltpu.VMEM((16, 16, TILE), jnp.float32),
             pltpu.SemaphoreType.DMA((STEPS,)),
             pltpu.SemaphoreType.DMA((1,)),
             *own_rows,

time: 133 us -> 134 us (level); the launches traced: 133 us -> 133 us
  Pallas kernels: 44.6 us -> 33.6 us
  waiting for transfers between devices: 30.9 us -> 39.8 us
  blocking collectives: 46.4 us -> 47.8 us
    pallas_call x2, Pallas kernels: 34.5 us -> 23.5 us  [batch_call(): pl.pallas_call(body, in_specs=[pl.BlockSpec(memory_space=pltpu.SMEM), pl....]
    all_to_all x2, waiting for transfers between devices: 30.9 us -> 39.8 us  [exchange(): return lax.all_to_all(value, ROW_COL, 0, 0, tiled=True)]
    all_to_all x2, blocking collectives: 46.4 us -> 47.8 us  [exchange(): return lax.all_to_all(value, ROW_COL, 0, 0, tiled=True)]
  transfers between devices with their start and end apart: 2 -> 2, of which waited for: 2 -> 2; matrix products, arithmetic and copies ran while one was open for 0% -> 0% of each run, Pallas kernels for 18% -> 11%
where the time goes in v6:
time: 134 us; the launch traced here: 133 us
  blocking collectives  47.8 us (36%)
  waiting for transfers between devices  39.8 us (30%)
  Pallas kernels  33.6 us (25%)
  starting transfers between devices  10.7 us (8%)
    all_to_all x2, blocking collectives, exchange(): return lax.all_to_all(value, ROW_COL, 0, 0, tiled=True)  47.8 us
    all_to_all x2, waiting for transfers between devices, exchange(): return lax.all_to_all(value, ROW_COL, 0, 0, tiled=True)  39.8 us
    pallas_call x2, Pallas kernels, batch_call(): pl.pallas_call(body, in_specs=[pl.BlockSpec(memory_space=pltpu.SMEM), pl....  23.5 us
    all_to_all x2, starting transfers between devices, exchange(): return lax.all_to_all(value, ROW_COL, 0, 0, tiled=True)  10.7 us
    pallas_call x1, Pallas kernels, spread(): pl.pallas_call(spread_body, out_shape=pltpu.VMEM((DEVICES * LINES, TILE),...  2.82 us
  transfers between devices with their start and end apart: 2, of which 2 were waited for; matrix products, arithmetic and copies ran while one was open for 0% of the time, Pallas kernels for 11%

profile of v6, /device:TPU:1, one launch (start us, length us, event | category | flops | bytes accessed | tf_op | source)
XLA Modules:
  0.0 132.6 jit_solution(14298029647115288054)
XLA Ops:
  0.6 2.8 %spread_rows.1 = bf16[3584,128]{1,0:T(8,128)(2,1)S(1)} custom-call(s32[2,7]{1,0:T(2,128)} %list_in.1, s32[2]{0:T(128)} %tiles_in.1, s32[2]{0:T(128)} %points_in.1, bf16[768,1536]{1,0:T(8,128)(2,1)} %first.1, bf16[768,1536]{1,0:T(8,128)(2,1)} %second.1), custom_call_target="tpu_custom_call" | custom-call | tf_op jit(solution)/shard_map/spread_rows/pallas_call | solution.py:103
  3.5 28.8 %all_to_all.20 = bf16[128,7,4,128]{3,2,1,0:T(4,128)(2,1)S(1)} all-to-all(bf16[128,7,4,128]{3,2,1,0:T(4,128)(2,1)S(1)} %bitcast.9), channel_id=1, replica_groups=mesh['row_0'=4,'row_1'=4,'col_0'=4,'col_1'=2] {'row_0','row_1','col_0','..., dimensions={0} | all-to-all | bytes 1835008 | tf_op jit(solution)/shard_map/all_to_all | solution.py:577
  32.2 2.3 %pick_windows.1 = (s32[64,56,128]{2,1,0:T(8,128)}, s32[768,128]{1,0:T(8,128)}, s32[8,128]{1,0:T(8,128)}, f32[8,128]{1,0:T(8,128)}) custom-call(bf16[3584,128]{1,0:T(8,128)(2,1)S(1)} %bitcast.10), custom_call_target="tpu_custom_call" | custom-call | tf_op jit(solution)/shard_map/pick_windows/pallas_call | solution.py:223
  34.6 4.7 %all-to-all-start.2 = ((s32[128,7,4,128]{3,2,1,0:T(4,128)}), s32[128,7,4,128]{3,2,1,0:T(4,128)S(1)}, u32[]{:S(2)}, u32[]{:S(2)}) async-start(s32[128,7,4,128]{3,2,1,0:T(4,128)} %bitcast.14), calls=%async_computation.2 | async-start | bytes 3670016 | tf_op jit(solution)/shard_map/all_to_all | solution.py:577
  39.3 1.5 %batch_tables.1.refs_0_ = s32[80]{0:T(128)} custom-call(s32[2,7]{1,0:T(2,128)} %list_in.1, s32[2]{0:T(128)} %tiles_in.1, s32[2]{0:T(128)} %points_in.1), custom_call_target="tpu_custom_call" | custom-call | tf_op jit(solution)/shard_map/batch_tables/pallas_call | solution.py:326
  40.8 2.5 %pick_rest.1 = s32[64,56,128]{2,1,0:T(8,128)} custom-call(s32[8,128]{1,0:T(8,128)} %get-tuple-element.10.starts, s32[768,128]{1,0:T(8,128)} %get-tuple-element.11.coded), custom_call_target="tpu_custom_call" | custom-call | tf_op jit(solution)/shard_map/pick_rest/pallas_call | solution.py:254
  43.2 23.4 %all-to-all-done.2 = s32[128,7,4,128]{3,2,1,0:T(4,128)S(1)} async-done(((s32[128,7,4,128]{3,2,1,0:T(4,128)}), s32[128,7,4,128]{3,2,1,0:T(4,128)S(1)}, u32[]{:S(2)}, u32[]{:S(2)}) %all-to-all-start.2) | async-done | bytes 1835040 | tf_op jit(solution)/shard_map/all_to_all | solution.py:577
  66.7 0.0 copy-start
  66.7 0.0 copy-start.1
  66.7 0.0 copy-start.2
  66.7 0.0 copy-start.3
  66.7 0.0 copy-start.4
  66.7 6.0 %all-to-all-start.1 = ((s32[128,7,4,128]{3,2,1,0:T(4,128)}), s32[128,7,4,128]{3,2,1,0:T(4,128)}, u32[]{:S(2)}, u32[]{:S(2)}) async-start(s32[128,7,4,128]{3,2,1,0:T(4,128)} %bitcast.13), calls=%async_computation.1 | async-start | bytes 3670016 | tf_op jit(solution)/shard_map/all_to_all | solution.py:577
  72.6 0.0 copy-done
  72.6 0.0 copy-done.1
  72.7 0.0 copy-done.2
  72.7 0.0 copy-done.3
  72.7 0.0 copy-done.4
  72.7 10.7 %batch_density_0.1 = (f32[2,4096]{1,0:T(2,128)S(1)}, f32[2,128]{1,0:T(2,128)S(1)}) custom-call(s32[80]{0:T(128)S(1)} %copy-done, s32[3584,128]{1,0:T(8,128)S(1)} %bitcast.11, f32[8,128]{1,0:T(8,128)S(1)} %copy-done.4, f32[3,2,4096]{2,1,0:T(2,128)S(1)} %copy-done.1, f32[2,4096]{1,0:T(2,128)S(1)} %copy-done.2, s32[2,4096]{1,0:T(2,128)S(1)} %copy-done.3, ...), custom_call_target="tpu_custom_call" | custom-call | flops 25999998976 | bytes 10000000 | tf_op jit(solution)/shard_map/batch_density_0/pallas_call | solution.py:509
  83.4 16.3 %all-to-all-done.1 = s32[128,7,4,128]{3,2,1,0:T(4,128)} async-done(((s32[128,7,4,128]{3,2,1,0:T(4,128)}), s32[128,7,4,128]{3,2,1,0:T(4,128)}, u32[]{:S(2)}, u32[]{:S(2)}) %all-to-all-start.1) | async-done | bytes 1835040 | tf_op jit(solution)/shard_map/all_to_all | solution.py:577
  99.7 12.8 %batch_density_1.1 = (f32[2,2,4096]{2,1,0:T(2,128)}, f32[128,2,128]{2,1,0:T(2,128)S(1)}) custom-call(s32[80]{0:T(128)S(1)} %copy-done, s32[3584,128]{1,0:T(8,128)} %bitcast.3.refs_1_, f32[2,128]{1,0:T(2,128)S(1)} %get-tuple-element.14.refs_2_, f32[2,4096]{1,0:T(2,128)S(1)} %get-tuple-element.15.refs_3_, f32[8,128]{1,0:T(8,128)S(1)} %copy-done.4, ...), custom_call_target="tpu_custom_call" | custom-call | flops 25999998976 | bytes 10000000 | tf_op jit(solution)/shard_map/batch_density_1/pallas_call | solution.py:509
  112.6 19.0 %all_to_all.21 = f32[128,2,128]{2,1,0:T(2,128)S(1)} all-to-all(f32[128,2,128]{2,1,0:T(2,128)S(1)} %get-tuple-element.17), channel_id=1, replica_groups=mesh['row_0'=4,'row_1'=4,'col_0'=4,'col_1'=2] {'row_0','row_1','col_0','..., dimensions={0} | all-to-all | bytes 262144 | tf_op jit(solution)/shard_map/all_to_all | solution.py:577
  131.6 1.0 moment_table.1
Async XLA Ops:
  34.6 32.1 %all-to-all-start.2 = ((s32[128,7,4,128]{3,2,1,0:T(4,128)}), s32[128,7,4,128]{3,2,1,0:T(4,128)S(1)}, u32[]{:S(2)}, u32[]{:S(2)}) async-start(s32[128,7,4,128]{3,2,1,0:T(4,128)} %bitcast.14), calls=%async_computation.2 | async-start | bytes 3670016 | tf_op jit(solution)/shard_map/all_to_all | solution.py:577
  66.7 6.0 %copy-start = (s32[80]{0:T(128)S(1)}, s32[80]{0:T(128)}, u32[]{:S(2)}) copy-start(s32[80]{0:T(128)} %batch_tables.1.refs_0_) | copy-start | bytes 964
  66.7 6.0 %copy-start.1 = (f32[3,2,4096]{2,1,0:T(2,128)S(1)}, f32[3,2,4096]{2,1,0:T(2,128)}, u32[]{:S(2)}) copy-start(f32[3,2,4096]{2,1,0:T(2,128)} %refs_5_.3) | copy-start | bytes 294916
  66.7 6.0 %copy-start.2 = (f32[2,4096]{1,0:T(2,128)S(1)}, f32[2,4096]{1,0:T(2,128)}, u32[]{:S(2)}) copy-start(f32[2,4096]{1,0:T(2,128)} %refs_6_.1) | copy-start | bytes 98308
  66.7 6.0 %copy-start.3 = (s32[2,4096]{1,0:T(2,128)S(1)}, s32[2,4096]{1,0:T(2,128)}, u32[]{:S(2)}) copy-start(s32[2,4096]{1,0:T(2,128)} %refs_7_.1) | copy-start | bytes 98308
  66.7 6.0 %copy-start.4 = (f32[8,128]{1,0:T(8,128)S(1)}, f32[8,128]{1,0:T(8,128)}, u32[]{:S(2)}) copy-start(f32[8,128]{1,0:T(8,128)} %get-tuple-element.13.refs_2_.refs_4_) | copy-start | bytes 12292
  66.7 33.0 %all-to-all-start.1 = ((s32[128,7,4,128]{3,2,1,0:T(4,128)}), s32[128,7,4,128]{3,2,1,0:T(4,128)}, u32[]{:S(2)}, u32[]{:S(2)}) async-start(s32[128,7,4,128]{3,2,1,0:T(4,128)} %bitcast.13), calls=%async_computation.1 | async-start | bytes 3670016 | tf_op jit(solution)/shard_map/all_to_all | solution.py:577
